TPU v7x, 512 devices: a 8x2x16 block of a 8x16x16 slice. The times are simulated.
512 devices in a mesh: group: 2 (over y), slab: 16 (over z), subj: 8 (over x), yslab: 2 (over core).
Axes of the slice: x: 8, y: 2, z: 16, core: 2. Of those that a mesh axis runs over, the one named last changes fastest.
The devices are a block of a 8x16x16 slice.
Arguments:
- subjects: bfloat16 [16, 256, 16, 256], P(('group', 'subj'), 'slab', 'yslab'), parts along dimension 0, may hold values from -6 to 6
- offsets: int32 [16, 3, 256, 16, 256], P(('group', 'subj'), None, 'slab', 'yslab'), parts along dimension 0, may hold values from -2 to 1
- template: float32 [512, 16, 256], P(('group', 'slab'), 'yslab'), parts along dimension 0, may hold values from -6 to 6
- control: float32 [16, 3, 67, 7, 128], P(('group', 'subj')), parts along dimension 0, may hold values from -8 to 8
Outputs:
- template_out: float32 [512, 16, 256], P(('group', 'slab'), 'yslab'), parts along dimension 0
- control_out: float32 [16, 3, 67, 7, 128], P(('group', 'subj')), parts along dimension 0
There are 2 independent parts, one for each index of `group`. A program takes and returns all parts, laid end to end along the dimension named above; each array names one. Nothing has to cross between parts.
All inputs are finite; a program needn't handle non-finite values.
Results may differ from a plain program's by a relative error of at most 0.00065.
Values may be sent and summed in bfloat16 or wider, within the bound.
A program may use at most 64 MiB of HBM per device.

v0:
```python
import jax
import jax.numpy as jnp
from jax import lax
from jax.sharding import PartitionSpec as P

KNOT = 4
KNOT_X = 2
HALO = 2
ITERS = 2


step_length = 0.5
tiny_term = 1e-06


def extended_2(value, sides, width):
    for axis, dim in sides:
        peers, length = (lax.axis_size(axis), value.shape[dim])
        up = [(i, (i + 1) % peers) for i in range(peers - 1)]
        down = [(j, i) for i, j in up]
        last = lax.slice_in_dim(value, length - width, length, axis=dim)
        initial = lax.slice_in_dim(value, 0, width, axis=dim)
        before = lax.ppermute(last, axis, up)
        after = lax.ppermute(initial, axis, down)
        value = jnp.concatenate([before, value, after], axis=dim)
    return value


def sent_to_all(value, axis):
    copies = jnp.broadcast_to(value, (lax.axis_size(axis), *value.shape))
    return lax.all_to_all(copies, axis, split_axis=0, concat_axis=0, tiled=True)


def taken_together(value, axis):
    everything = sent_to_all(value, axis)
    return jnp.sum(everything, axis=0)


def over_pieces(value, axis):
    return lax.all_gather(value, axis).astype(jnp.float32).sum(0)


def shifted(block, axis, distance):
    devices = range(lax.axis_size(axis))
    route = [(i - distance, i) for i in devices if i - distance in devices]
    return lax.ppermute(block, axis, route)


def laid_out(pieces, dim):
    pieces = jnp.moveaxis(pieces, 0, dim)
    dims = pieces.shape
    return pieces.reshape(*dims[:dim], dims[dim] * dims[dim + 1], *dims[dim + 2 :])


def collect(value, axis, dim):
    return laid_out(sent_to_all(value, axis), dim)


def broadcast(value, axis, root):
    return lax.dynamic_index_in_dim(lax.all_gather(value, axis), root, 0, keepdims=False)


def basis(positions, columns, spacing, wrap):
    cell = positions // spacing
    frac = (positions - cell * spacing).astype(jnp.float32) / spacing
    weights = [
        (1.0 - frac) ** 3 / 6.0,
        (3.0 * frac**3 - 6.0 * frac**2 + 4.0) / 6.0,
        (-3.0 * frac**3 + 3.0 * frac**2 + 3.0 * frac + 1.0) / 6.0,
        frac**3 / 6.0,
    ]
    index = jnp.arange(columns, dtype=jnp.int32)
    matrix = jnp.zeros((positions.shape[0], columns), jnp.float32)
    for offset in range(4):
        target = cell + offset
        if wrap:
            target = target % columns
        matrix = matrix + jnp.where(
            index[None, :] == target[:, None], weights[offset][:, None], 0.0
        )
    return matrix


def forward_field(coeffs, basis_z, basis_y, basis_x):
    high = lax.Precision.HIGHEST
    first = jnp.einsum("cabg,za->czbg", coeffs, basis_z, precision=high)
    second = jnp.einsum("czbg,yb->czyg", first, basis_y, precision=high)
    return jnp.einsum("czyg,xg->czyx", second, basis_x, precision=high)


def adjoint_field(gradient, basis_z, basis_y, basis_x):
    high = lax.Precision.HIGHEST
    first = jnp.einsum("czyx,xg->czyg", gradient, basis_x, precision=high)
    second = jnp.einsum("czyg,yb->czbg", first, basis_y, precision=high)
    return jnp.einsum("czbg,za->cabg", second, basis_z, precision=high)


def choose(shift_of, table, lead):
    result = table[-HALO + lead]
    for value in range(-HALO + 1, HALO):
        result = jnp.where(shift_of == value, table[value + lead], result)
    return result


def trilinear_local(volume, shifts, fraction, depth, height, width):
    frac_z, frac_y, frac_x = (fraction[0], fraction[1], fraction[2])
    shift_z, shift_y, shift_x = (shifts[0], shifts[1], shifts[2])
    along_y_of = {}
    diff_y_of = {}
    diff_xy_of = {}
    for move_z in range(-HALO, HALO + 1):
        along_x_of = {}
        diff_x_of = {}
        for move_y in range(-HALO, HALO + 1):
            plane = volume[
                move_z + HALO : move_z + HALO + depth, move_y + HALO : move_y + HALO + height, :
            ].astype(jnp.float32)
            columns = {}
            for move_x in range(-HALO, HALO + 1):
                columns[move_x] = plane[:, :, move_x + HALO : move_x + HALO + width]
            low = choose(shift_x, columns, 0)
            high = choose(shift_x, columns, 1)
            along_x_of[move_y] = low * (1.0 - frac_x) + high * frac_x
            diff_x_of[move_y] = high - low
        along_low = choose(shift_y, along_x_of, 0)
        along_high = choose(shift_y, along_x_of, 1)
        diff_low = choose(shift_y, diff_x_of, 0)
        diff_high = choose(shift_y, diff_x_of, 1)
        along_y_of[move_z] = along_low * (1.0 - frac_y) + along_high * frac_y
        diff_y_of[move_z] = along_high - along_low
        diff_xy_of[move_z] = diff_low * (1.0 - frac_y) + diff_high * frac_y
    along_y = [choose(shift_z, along_y_of, 0), choose(shift_z, along_y_of, 1)]
    diff_y = [choose(shift_z, diff_y_of, 0), choose(shift_z, diff_y_of, 1)]
    diff_xy = [choose(shift_z, diff_xy_of, 0), choose(shift_z, diff_xy_of, 1)]
    warped = along_y[0] * (1.0 - frac_z) + along_y[1] * frac_z
    slope_z = along_y[1] - along_y[0]
    slope_y = diff_y[0] * (1.0 - frac_z) + diff_y[1] * frac_z
    slope_x = diff_xy[0] * (1.0 - frac_z) + diff_xy[1] * frac_z
    return (warped, jnp.stack([slope_z, slope_y, slope_x]))


def shards(subjects, offsets, template, control):
    local_subjects = subjects.shape[0]
    depth, height, width = (subjects.shape[1], subjects.shape[2], subjects.shape[3])
    rows_slab = depth // KNOT
    cohort = local_subjects * lax.axis_size("subj")
    extended = extended_2(subjects, (("slab", 1), ("yslab", 2)), HALO)
    extended = jnp.pad(extended, ((0, 0), (0, 0), (0, 0), (HALO, HALO)))
    basis_z = basis(jnp.arange(depth, dtype=jnp.int32), rows_slab + 3, KNOT, False)
    y_start = lax.axis_index("yslab") * height
    basis_y = basis(y_start + jnp.arange(height, dtype=jnp.int32), control.shape[3], KNOT, False)
    basis_x = basis(jnp.arange(width, dtype=jnp.int32), control.shape[4], KNOT_X, True)
    first_row = lax.axis_index("slab") * rows_slab
    current = template
    coeffs_all = control
    for iteration in range(ITERS):
        band_coeffs = lax.dynamic_slice_in_dim(coeffs_all[0], first_row, rows_slab + 3, 1)
        displace = forward_field(band_coeffs, basis_z, basis_y, basis_x)
        tanh_u = jnp.tanh(displace)
        fraction = 0.5 + 0.5 * tanh_u
        warped, slopes = trilinear_local(extended[0], offsets[0], fraction, depth, height, width)
        resid = warped - current
        grad_u = resid[None] * slopes * (1.0 - tanh_u * tanh_u)
        band_list = [adjoint_field(grad_u, basis_z, basis_y, basis_x)]
        band_grid = jnp.stack(band_list)
        current = taken_together(warped, "subj") / cohort
        band_grid = over_pieces(band_grid.astype(jnp.bfloat16), "yslab").astype(jnp.float32)
        head_rows = band_grid[:, :, :rows_slab]
        tail_part = band_grid[:, :, rows_slab:]
        carried = shifted(tail_part, "slab", 1)
        head_rows = head_rows.at[:, :, :3].add(carried)
        owned = collect(head_rows.astype(jnp.bfloat16), "slab", 2).astype(head_rows.dtype)
        last_part = broadcast(tail_part, "slab", lax.axis_size("slab") - 1)
        grid = jnp.concatenate([owned, last_part], axis=2)
        lengths = jnp.sqrt(jnp.sum(grid * grid, axis=1))
        peak = jnp.max(lengths, axis=(1, 2, 3))
        coeffs_all = coeffs_all - step_length * grid / (peak[:, None, None, None, None] + tiny_term)
    return (current, coeffs_all)


def solution(mesh):
    in_specs = (
        P(("group", "subj"), "slab", "yslab", None),
        P(("group", "subj"), None, "slab", "yslab", None),
        P(("group", "slab"), "yslab", None),
        P(("group", "subj"), None, None, None, None),
    )
    out_specs = (P(("group", "slab"), "yslab", None), P(("group", "subj"), None, None, None, None))
    return jax.shard_map(shards, mesh=mesh, in_specs=in_specs, out_specs=out_specs, check_vma=False)
```

profile of v0, /device:TPU:82, one launch (start us, length us, event | category | flops | bytes accessed | tf_op | source)
XLA Modules:
  0.0 247.0 jit_solution(13805713560270818522)
XLA Ops:
  1.3 1.3 collective-permute-start.1
  2.7 6.7 %collective-permute-start = (bf16[1,2,8,256]{3,2,1,0:T(8,128)(2,1)S(1)}, bf16[1,2,8,256]{3,2,1,0:T(8,128)(2,1)S(1)}, u32[]{:S(2)}, u32[]{:S(2)}) collective-permute-start(bf16[1,2,8,256]{3,2,1,0:T(8,128)(2,1)S(1)} %get-tuple-element.161), channel_id=1, source_target_pairs={{0,16},{16,32},{32,48},{48,64},{64,80},{80,96},{96,112},{112,128},... | collective-permute-start | bytes 24584 | tf_op jit(solution)/shard_map/ppermute | solution.py:23
  14.9 1.1 convolution_bitcast_fusion.5
  16.0 1.1 convolution_bitcast_fusion.3
  17.7 1.6 collective-permute-start.2
  19.3 1.3 collective-permute-start.3
  20.6 1.4 multiply_add_fusion.1
  25.9 3.3 %fusion.331 = (f32[16,8,256]{2,1,0:T(8,128)S(1)}, f32[16,8,256]{2,1,0:T(8,128)S(1)}, f32[16,8,256]{2,1,0:T(8,128)S(1)}, f32[16,8,256]{2,1,0:T(8,128)S(1)}, f32[1...) fusion(f32[16,8,256]{2,1,0:T(8,128)S(1)} %copy-done.55, ...), kind=kLoop, calls=%fused_computation.601 | loop fusion | flops 8093696 | bytes 21266432 | tf_op jit(solution)/shard_map/sub | solution.py:162
  31.2 2.9 %add_bitcast_fusion.2 = (f32[1,16,8,256]{3,2,1,0:T(8,128)S(1)}, f32[16,8,256]{2,1,0:T(8,128)}, f32[16,8,256]{2,1,0:T(8,128)}, f32[16,8,256]{2,1,0:T(8,128)}, f32...) fusion(pred[1,1,16,8,256]{4,3,2,1,0:T(8,128)(4,1)S(1)} %get-tup, ...), kind=kLoop, calls=%fused_computation.254 | loop fusion | flops 2654208 | bytes 8454144 | tf_op jit(solution)/shard_map/stack | solution.py:139
  34.1 1.4 fusion.4
  37.5 2.4 all-gather
  39.9 6.0 %collective-permute-start.4 = (f32[1,3,3,7,128]{4,2,3,1,0:T(4,128)S(1)}, f32[1,3,3,7,128]{4,2,3,1,0:T(4,128)S(1)}, u32[]{:S(2)}, u32[]{:S(2)}) collective-permute-start(f32[1,3,3,7,128]{4,2,3,1,0:T(4,128)S(1)} %slice.1057), channel_id=1, source_target_pairs={{0,16},{16,32},{32,48},{48,64},{64,80},{80,96},{96,112},{112,128},... | collective-permute-start | bytes 96776 | tf_op jit(solution)/shard_map/ppermute | solution.py:46
  45.9 1.7 collective-permute-done.4
  48.6 38.6 %all-to-all-start = ((bf16[16,1,3,4,7,128]{5,3,4,2,1,0:T(4,128)(2,1)}), bf16[16,1,3,4,7,128]{5,3,4,2,1,0:T(4,128)(2,1)S(1)}, u32[]{:S(2)}, u32[]{:S(2)}) async-start(bf16[16,1,3,4,7,128]{5,3,4,2,1,0:T(4,128)(2,1)} %broadcast_in_dim.205), calls=%async_computation | async-start | bytes 688128 | tf_op jit(solution)/shard_map/all_to_all | solution.py:31
  87.3 20.7 %all-to-all-done = bf16[16,1,3,4,7,128]{5,3,4,2,1,0:T(4,128)(2,1)S(1)} async-done(((bf16[16,1,3,4,7,128]{5,3,4,2,1,0:T(4,128)(2,1)}), bf16[16,1,3,4,7,128]{5,3,4,2,1,0:T(4,128)(2,1)S(1)}, u32[]{:S(2)}, u32[]{:S(2)}) %all-to-all-start) | async-done | bytes 344096 | tf_op jit(solution)/shard_map/all_to_all | solution.py:31
  108.0 1.1 broadcast_in_dim.207
  109.2 7.7 %all-to-all-start.2 = ((f32[8,16,8,256]{3,2,1,0:T(8,128)}), f32[8,16,8,256]{3,2,1,0:T(8,128)S(1)}, u32[]{:S(2)}, u32[]{:S(2)}) async-start(f32[8,16,8,256]{3,2,1,0:T(8,128)} %broadcast_in_dim.207), calls=%async_computation.2 | async-start | bytes 2097152 | tf_op jit(solution)/shard_map/all_to_all | solution.py:31
  116.9 32.0 %all-gather.1 = f32[16,3,3,7,128]{4,3,2,1,0:T(8,128)S(1)} all-gather(f32[1,3,3,7,128]{4,3,2,1,0:T(8,128)S(1)} %copy.71), channel_id=3, replica_groups=mesh['group'=2,'slab'=16,'subj'=8,'yslab'=2] {'slab'}, dimensions={0}, use_global_device_ids=true | all-gather | bytes 548352 | tf_op jit(solution)/shard_map/all_gather | solution.py:60
  150.9 1.2 copy_subtract_fusion
  152.1 1.1 convolution_bitcast_fusion.4
  153.2 1.2 convolution_bitcast_fusion.1
  154.5 2.3 multiply_add_fusion
  158.6 3.4 %multiply_subtract_fusion = (f32[16,8,256]{2,1,0:T(8,128)S(1)}, f32[16,8,256]{2,1,0:T(8,128)S(1)}, f32[16,8,256]{2,1,0:T(8,128)S(1)}, f32[16,8,256]{2,1,0:T(8,12...) fusion(f32[16,8,256]{2,1,0:T(8,128)} %reduce_sum.62, ...), kind=kLoop, calls=%fused_computation.198 | loop fusion | flops 4390912 | bytes 9109504 | tf_op jit(solution)/shard_map/sub | solution.py:162
  163.1 1.4 fusion.11
  166.5 1.9 all-gather.2
  168.5 2.5 %collective-permute-start.5 = (f32[1,3,3,7,128]{4,2,3,1,0:T(4,128)S(1)}, f32[1,3,3,7,128]{4,2,3,1,0:T(4,128)S(1)}, u32[]{:S(2)}, u32[]{:S(2)}) collective-permute-start(f32[1,3,3,7,128]{4,2,3,1,0:T(4,128)S(1)} %slice.1064), channel_id=1, source_target_pairs={{0,16},{16,32},{32,48},{48,64},{64,80},{80,96},{96,112},{112,128},... | collective-permute-start | bytes 96776 | tf_op jit(solution)/shard_map/ppermute | solution.py:46
  171.0 1.7 collective-permute-done.5
  172.9 29.6 %all_to_all.20 = bf16[16,1,3,4,7,128]{5,3,4,2,1,0:T(4,128)(2,1)S(1)} all-to-all(bf16[16,1,3,4,7,128]{5,3,4,2,1,0:T(4,128)(2,1)S(1)} %broadcast_in_dim.208), channel_id=1, replica_groups=mesh['group'=2,'slab'=16,'subj'=8,'yslab'=2] {'slab'}, dimensions={0} | all-to-all | bytes 688128 | tf_op jit(solution)/shard_map/all_to_all | solution.py:31
  202.5 1.1 broadcast_in_dim.206
  203.6 7.5 %all-to-all-start.1 = ((f32[8,16,8,256]{3,2,1,0:T(8,128)}), f32[8,16,8,256]{3,2,1,0:T(8,128)S(1)}, u32[]{:S(2)}, u32[]{:S(2)}) async-start(f32[8,16,8,256]{3,2,1,0:T(8,128)} %broadcast_in_dim.206), calls=%async_computation.1 | async-start | bytes 2097152 | tf_op jit(solution)/shard_map/all_to_all | solution.py:31
  211.1 31.8 %all-gather.3 = f32[16,3,3,7,128]{4,3,2,1,0:T(8,128)S(1)} all-gather(f32[1,3,3,7,128]{4,3,2,1,0:T(8,128)S(1)} %copy.80), channel_id=5, replica_groups=mesh['group'=2,'slab'=16,'subj'=8,'yslab'=2] {'slab'}, dimensions={0}, use_global_device_ids=true | all-gather | bytes 548352 | tf_op jit(solution)/shard_map/all_gather | solution.py:60
  244.7 1.6 copy.82
  (189 shorter events, 23.7 us)
Async XLA Ops:
  1.3 16.3 %collective-permute-start.1 = (bf16[1,2,8,256]{3,2,1,0:T(8,128)(2,1)S(1)}, bf16[1,2,8,256]{3,2,1,0:T(8,128)(2,1)S(1)}, u32[]{:S(2)}, u32[]{:S(2)}) collective-permute-start(bf16[1,2,8,256]{3,2,1,0:T(8,128)(2,1)S(1)} %get-tuple-element.160), channel_id=1, source_target_pairs={{16,0},{32,16},{48,32},{64,48},{80,64},{96,80},{112,96},{128,112},... | collective-permute-start | bytes 24584 | tf_op jit(solution)/shard_map/ppermute | solution.py:24
  2.7 15.0 %collective-permute-start = (bf16[1,2,8,256]{3,2,1,0:T(8,128)(2,1)S(1)}, bf16[1,2,8,256]{3,2,1,0:T(8,128)(2,1)S(1)}, u32[]{:S(2)}, u32[]{:S(2)}) collective-permute-start(bf16[1,2,8,256]{3,2,1,0:T(8,128)(2,1)S(1)} %get-tuple-element.161), channel_id=1, source_target_pairs={{0,16},{16,32},{32,48},{48,64},{64,80},{80,96},{96,112},{112,128},... | collective-permute-start | bytes 24584 | tf_op jit(solution)/shard_map/ppermute | solution.py:23
  16.0 1.7 copy-start.56
  17.7 4.3 %collective-permute-start.2 = (bf16[1,20,2,256]{3,2,1,0:T(2,128)(2,1)S(1)}, bf16[1,20,2,256]{3,2,1,0:T(2,128)(2,1)S(1)}, u32[]{:S(2)}, u32[]{:S(2)}) collective-permute-start(bf16[1,20,2,256]{3,2,1,0:T(2,128)(2,1)S(1)} %get-tuple-element.158), channel_id=1, source_target_pairs={{0,1},{2,3},{4,5},{6,7},{8,9},{10,11},{12,13},{14,15},{16,17},{18,... | collective-permute-start | bytes 61448 | tf_op jit(solution)/shard_map/ppermute | solution.py:23
  19.3 3.1 %collective-permute-start.3 = (bf16[1,20,2,256]{3,2,1,0:T(2,128)(2,1)S(1)}, bf16[1,20,2,256]{3,2,1,0:T(2,128)(2,1)S(1)}, u32[]{:S(2)}, u32[]{:S(2)}) collective-permute-start(bf16[1,20,2,256]{3,2,1,0:T(2,128)(2,1)S(1)} %get-tuple-element.159), channel_id=1, source_target_pairs={{1,0},{3,2},{5,4},{7,6},{9,8},{11,10},{13,12},{15,14},{17,16},{19,... | collective-permute-start | bytes 61448 | tf_op jit(solution)/shard_map/ppermute | solution.py:24
  24.8 4.8 %copy-start = (f32[16,8,256]{2,1,0:T(8,128)}, f32[16,8,256]{2,1,0:T(8,128)S(1)}, u32[]{:S(2)}) copy-start(f32[16,8,256]{2,1,0:T(8,128)S(1)} %get-tuple-element.119) | copy-start | bytes 393220
  24.9 4.8 %copy-start.2 = (f32[16,8,256]{2,1,0:T(8,128)}, f32[16,8,256]{2,1,0:T(8,128)S(1)}, u32[]{:S(2)}) copy-start(f32[16,8,256]{2,1,0:T(8,128)S(1)} %get-tuple-element.154) | copy-start | bytes 393220
  24.9 4.8 %copy-start.4 = (f32[16,8,256]{2,1,0:T(8,128)}, f32[16,8,256]{2,1,0:T(8,128)S(1)}, u32[]{:S(2)}) copy-start(f32[16,8,256]{2,1,0:T(8,128)S(1)} %get-tuple-element.155) | copy-start | bytes 393220
  25.2 4.5 %copy-start.5 = (f32[16,8,256]{2,1,0:T(8,128)}, f32[16,8,256]{2,1,0:T(8,128)S(1)}, u32[]{:S(2)}) copy-start(f32[16,8,256]{2,1,0:T(8,128)S(1)} %get-tuple-element.120) | copy-start | bytes 393220
  25.2 4.5 %copy-start.6 = (f32[16,8,256]{2,1,0:T(8,128)}, f32[16,8,256]{2,1,0:T(8,128)S(1)}, u32[]{:S(2)}) copy-start(f32[16,8,256]{2,1,0:T(8,128)S(1)} %get-tuple-element.121) | copy-start | bytes 393220
  25.2 4.5 %copy-start.7 = (f32[16,8,256]{2,1,0:T(8,128)}, f32[16,8,256]{2,1,0:T(8,128)S(1)}, u32[]{:S(2)}) copy-start(f32[16,8,256]{2,1,0:T(8,128)S(1)} %get-tuple-element.156) | copy-start | bytes 393220
  25.3 4.5 %copy-start.8 = (f32[16,8,256]{2,1,0:T(8,128)}, f32[16,8,256]{2,1,0:T(8,128)S(1)}, u32[]{:S(2)}) copy-start(f32[16,8,256]{2,1,0:T(8,128)S(1)} %get-tuple-element.157) | copy-start | bytes 393220
  29.5 1.6 copy-start.36
  29.5 1.6 copy-start.37
  29.5 1.7 copy-start.38
  29.5 1.7 copy-start.39
  29.5 1.7 copy-start.40
  39.9 7.7 %collective-permute-start.4 = (f32[1,3,3,7,128]{4,2,3,1,0:T(4,128)S(1)}, f32[1,3,3,7,128]{4,2,3,1,0:T(4,128)S(1)}, u32[]{:S(2)}, u32[]{:S(2)}) collective-permute-start(f32[1,3,3,7,128]{4,2,3,1,0:T(4,128)S(1)} %slice.1057), channel_id=1, source_target_pairs={{0,16},{16,32},{32,48},{48,64},{64,80},{80,96},{96,112},{112,128},... | collective-permute-start | bytes 96776 | tf_op jit(solution)/shard_map/ppermute | solution.py:46
  48.6 59.4 %all-to-all-start = ((bf16[16,1,3,4,7,128]{5,3,4,2,1,0:T(4,128)(2,1)}), bf16[16,1,3,4,7,128]{5,3,4,2,1,0:T(4,128)(2,1)S(1)}, u32[]{:S(2)}, u32[]{:S(2)}) async-start(bf16[16,1,3,4,7,128]{5,3,4,2,1,0:T(4,128)(2,1)} %broadcast_in_dim.205), calls=%async_computation | async-start | bytes 688128 | tf_op jit(solution)/shard_map/all_to_all | solution.py:31
  109.2 48.5 %all-to-all-start.2 = ((f32[8,16,8,256]{3,2,1,0:T(8,128)}), f32[8,16,8,256]{3,2,1,0:T(8,128)S(1)}, u32[]{:S(2)}, u32[]{:S(2)}) async-start(f32[8,16,8,256]{3,2,1,0:T(8,128)} %broadcast_in_dim.207), calls=%async_computation.2 | async-start | bytes 2097152 | tf_op jit(solution)/shard_map/all_to_all | solution.py:31
  153.2 3.5 %copy-start.48 = (f32[16,8,256]{2,1,0:T(8,128)S(1)}, f32[16,8,256]{2,1,0:T(8,128)}, u32[]{:S(2)}) copy-start(f32[16,8,256]{2,1,0:T(8,128)} %get-tuple-element.109) | copy-start | bytes 393220
  153.2 3.5 %copy-start.49 = (f32[16,8,256]{2,1,0:T(8,128)S(1)}, f32[16,8,256]{2,1,0:T(8,128)}, u32[]{:S(2)}) copy-start(f32[16,8,256]{2,1,0:T(8,128)} %get-tuple-element.110) | copy-start | bytes 393220
  153.2 3.5 %copy-start.50 = (f32[16,8,256]{2,1,0:T(8,128)S(1)}, f32[16,8,256]{2,1,0:T(8,128)}, u32[]{:S(2)}) copy-start(f32[16,8,256]{2,1,0:T(8,128)} %get-tuple-element.111) | copy-start | bytes 393220
  154.4 2.3 copy-start.41
  154.4 2.3 copy-start.42
  154.4 2.3 copy-start.43
  154.4 2.3 copy-start.44
  154.4 2.3 copy-start.45
  154.5 2.3 copy-start.46
  154.5 2.3 copy-start.47
  168.5 4.2 %collective-permute-start.5 = (f32[1,3,3,7,128]{4,2,3,1,0:T(4,128)S(1)}, f32[1,3,3,7,128]{4,2,3,1,0:T(4,128)S(1)}, u32[]{:S(2)}, u32[]{:S(2)}) collective-permute-start(f32[1,3,3,7,128]{4,2,3,1,0:T(4,128)S(1)} %slice.1064), channel_id=1, source_target_pairs={{0,16},{16,32},{32,48},{48,64},{64,80},{80,96},{96,112},{112,128},... | collective-permute-start | bytes 96776 | tf_op jit(solution)/shard_map/ppermute | solution.py:46
  203.6 42.7 %all-to-all-start.1 = ((f32[8,16,8,256]{3,2,1,0:T(8,128)}), f32[8,16,8,256]{3,2,1,0:T(8,128)S(1)}, u32[]{:S(2)}, u32[]{:S(2)}) async-start(f32[8,16,8,256]{3,2,1,0:T(8,128)} %broadcast_in_dim.206), calls=%async_computation.1 | async-start | bytes 2097152 | tf_op jit(solution)/shard_map/all_to_all | solution.py:31
  (34 other events, 36.8 us)
where the time goes:
time: 248 us; the launch traced here: 247 us
  blocking collectives  97.6 us (39%)
  starting transfers between devices  73.2 us (30%)
  waiting for transfers between devices  24.4 us (10%)
  other arithmetic  22.3 us (9%)
  matrix products  14.8 us (6%)
  local copies, waits for them, and re-layouts  11.8 us (5%)
  between operations  2.92 us (1%)
    all_gather x2, blocking collectives, broadcast(): lax.all_gather(value, axis)  63.7 us
    all_to_all x3, starting transfers between devices, sent_to_all(): return lax.all_to_all(copies, axis, split_axis=0, concat_axis=0, tiled=True)  53.9 us
    all_to_all x1, blocking collectives, sent_to_all(): return lax.all_to_all(copies, axis, split_axis=0, concat_axis=0, tiled=True)  29.6 us
    all_to_all x3, waiting for transfers between devices, sent_to_all(): return lax.all_to_all(copies, axis, split_axis=0, concat_axis=0, tiled=True)  20.7 us
    ppermute x2, starting transfers between devices, shifted(): return lax.ppermute(block, axis, route)  8.51 us
    ppermute x2, starting transfers between devices, extended_2(): before = lax.ppermute(last, axis, up)  8.23 us
    sub x2, other arithmetic, shards(): resid = warped - current  6.69 us
    unnamed x121, local copies, waits for them, and re-layouts  6.15 us
  transfers between devices with their start and end apart: 9, of which 4 were waited for; matrix products, arithmetic and copies ran while one was open for 8% of the time, Pallas kernels for 0%

commit v1 on v0

v1 whole, which is shorter than its diff:
```python
import jax
import jax.numpy as jnp
import numpy as np
from jax import lax
from jax.experimental import pallas as pl
from jax.experimental.pallas import tpu as pltpu
from jax.sharding import PartitionSpec as P

KNOT = 4
HALO = 2
STEP = 0.5
TINY = 1e-06
CUBE = 384.0
CUBE_X = 48.0
SCALE = 1.0 / (CUBE * CUBE * CUBE_X)
F32 = jnp.float32
BF16 = jnp.bfloat16
MESH = pl.DeviceIdType.MESH


def spline(count, columns, spacing, wrap):
    whole = 6 * spacing**3
    matrix = np.zeros((count, columns))
    for t in range(count):
        j = t // spacing
        s = (t - j * spacing) / spacing
        weights = [
            (1 - s) ** 3 / 6,
            (3 * s**3 - 6 * s**2 + 4) / 6,
            (-3 * s**3 + 3 * s**2 + 3 * s + 1) / 6,
            s**3 / 6,
        ]
        for o in range(4):
            column = (j + o) % columns if wrap else j + o
            matrix[t, column] += weights[o] * whole
    return np.rint(matrix)


def halves(whole):
    high = np.asarray(whole, np.float32).astype(BF16).astype(np.float32)
    low = (whole - high).astype(np.float32)
    assert (low.astype(BF16).astype(np.float32) == low).all()
    return high, low


def constants(depth, height, width, columns_x):
    assert (depth, height) == (16, 8)
    bz = spline(depth, 7, KNOT, False)
    by = spline(height, 5, KNOT, False)
    forward = np.zeros((2, depth, height, 8, 8))
    for k in range(2):
        forward[k, :, :, :7, 2 * k : 2 * k + 5] = np.einsum("za,yb->zyab", bz, by)
    forward = forward.reshape(2, depth * height, 64)
    high, low = halves(forward)
    forward = np.concatenate([high, low, high], axis=2)
    adjoint = np.zeros((3, 16, depth, height))
    for group, rows in enumerate(([0, 1, 2], [4, 5, 6], [3])):
        for place, a in enumerate(rows):
            for b in range(5):
                adjoint[group, place * 5 + b] = np.outer(bz[:, a], by[:, b])
    adjoint = adjoint.reshape(48, depth * height)
    high, low = halves(adjoint)
    adjoint = np.concatenate([high, low, high], axis=1)
    gather = np.zeros((3, 64, 10, 16))
    for edge in range(3):
        for a in range(7):
            for b in range(7):
                for k in range(2):
                    c = b - 2 * k
                    if not 0 <= c < 5:
                        continue
                    row = a * 8 + b
                    if a < 3:
                        gather[edge, row, 3 * k, a * 5 + c] = 1
                        if edge != 1:
                            gather[edge, row, 6 + k, a * 5 + c] = 1
                    elif a == 3:
                        gather[edge, row, 3 * k + 2, c] = 1
                    else:
                        gather[edge, row, 3 * k + 1, (a - 4) * 5 + c] = 1
                        if edge != 2:
                            gather[edge, row, 8 + k, (a - 4) * 5 + c] = 1
    gather = gather.reshape(3, 64, 160)
    bx = spline(width, columns_x, 2, True)
    across = np.concatenate([bx.T, bx.T], axis=0)
    return [jnp.asarray(m, BF16) for m in (forward, across, bx, adjoint, gather)]


def split(x):
    high = x.astype(BF16)
    return high, (x - high.astype(F32)).astype(BF16)


def dot(a, b):
    return jnp.dot(a, b, preferred_element_type=F32)


def field(coeffs, wf, bxt, out):
    for c in range(3):
        high, low = split(coeffs[c])
        first = dot(wf, jnp.concatenate([high, high, low], axis=0))
        high, low = split(first)
        out[c] = dot(jnp.concatenate([high, low], axis=1), bxt) * SCALE


def send(src, dst, send_sem, recv_sem, **where):
    return pltpu.make_async_remote_copy(
        src_ref=src,
        dst_ref=dst,
        send_sem=send_sem,
        recv_sem=recv_sem,
        device_id=where,
        device_id_type=MESH,
    )


def greet(barrier, **where):
    pl.semaphore_signal(barrier, inc=1, device_id=where, device_id_type=MESH)


def each(first, last, body):
    def step(i, carry):
        body(i)
        return carry

    lax.fori_loop(first, last, step, 0)


def halo_kernel(
    slabs, subject, control, wf, bxt, own_out, peer_out, u_out,
    own, peer, band, coeffs, band_sem, send_sem, recv_sem,
):
    me = lax.axis_index("slab")
    core = lax.axis_index("yslab")
    depth = subject.shape[0]
    up = lax.rem(me + 1, slabs)
    down = lax.rem(me + slabs - 1, slabs)
    other = 1 - core
    barrier = pltpu.get_barrier_semaphore()
    greet(barrier, yslab=other)
    for slab in (up, down):
        greet(barrier, slab=slab)
        greet(barrier, slab=slab, yslab=other)
    fetch = pltpu.make_async_copy(control.at[:, pl.ds(me * (depth // KNOT), 7)], band, band_sem)
    fetch.start()
    coeffs[...] = jnp.zeros_like(coeffs)
    pl.semaphore_wait(barrier, 5)
    inner = pl.ds(HALO, depth)
    low = pl.ds(0, HALO)
    high = pl.ds(depth + HALO, HALO)
    first = pl.ds(0, HALO)
    last = pl.ds(depth - HALO, HALO)
    plan = [
        (subject, peer.at[inner], dict(yslab=other)),
        (subject.at[last], own.at[low], dict(slab=up)),
        (subject.at[last], peer.at[low], dict(slab=up, yslab=other)),
        (subject.at[first], own.at[high], dict(slab=down)),
        (subject.at[first], peer.at[high], dict(slab=down, yslab=other)),
    ]
    copies = [
        send(src, dst, send_sem.at[i], recv_sem.at[i], **where)
        for i, (src, dst, where) in enumerate(plan)
    ]
    for copy in copies[1:] + copies[:1]:
        copy.start()
    own_out[HALO : HALO + depth] = subject[...]
    fetch.wait()
    for c in range(3):
        coeffs[c, 0:7, 0:7, :] = band[c]
    field([coeffs[c].reshape(64, 128) for c in range(3)], wf[core], bxt[...], u_out)
    for copy in copies:
        copy.wait()
    own_out[0:HALO] = own[0:HALO]
    own_out[HALO + depth :] = own[HALO + depth :]
    peer_out[...] = peer[...]


def pick(shift, values):
    odd, top = shift
    steps = [jnp.where(odd, values[i + 1], values[i]) for i in range(4)]
    return jnp.where(top, steps[2], steps[0]), jnp.where(top, steps[3], steps[1])


def pick_many(shift, groups):
    pairs = [pick(shift, values) for values in zip(*groups)]
    return [p[0] for p in pairs], [p[1] for p in pairs]


def warp(lows, steps, u, current):
    th = [jnp.tanh(x) for x in u]
    fz, fy, fx = [0.5 + 0.5 * t for t in th]
    along = [low + fx * step for low, step in zip(lows, steps)]
    slope_y = [along[1] - along[0], along[3] - along[2]]
    along_y = [along[0] + fy * slope_y[0], along[2] + fy * slope_y[1]]
    slope_x = [steps[0] + fy * (steps[1] - steps[0]), steps[2] + fy * (steps[3] - steps[2])]
    slopes = [
        along_y[1] - along_y[0],
        slope_y[0] + fz * (slope_y[1] - slope_y[0]),
        slope_x[0] + fz * (slope_x[1] - slope_x[0]),
    ]
    warped = along_y[0] + fz * slopes[0]
    resid = warped - current
    return warped, [resid * slope * (1.0 - t * t) for slope, t in zip(slopes, th)]


def main_kernel(
    slabs, cohort, own, peer, u0, offsets, template, wf, bxt, bx, wa, gather,
    total_out, delta_out,
    shifted, corners, grad, warped, current, moved, terms, grid, parts,
    small, piece, summed, pieces, means, wide, wide_means, peaks, mine,
    ex_send, ex_recv, pk_send, pk_recv, rs_send, rs_recv, tg_send, tg_recv,
    ag_send, ag_recv, fw_send, fw_recv, tl_send, tl_recv,
):
    me = lax.axis_index("slab")
    core = lax.axis_index("yslab")
    who = lax.axis_index("subj")
    other = 1 - core
    up = lax.rem(me + 1, slabs)
    down = lax.rem(me + slabs - 1, slabs)
    depth = offsets.shape[1]
    share = depth // cohort * 8
    barrier = pltpu.get_barrier_semaphore()
    each(1, slabs, lambda d: greet(barrier, slab=lax.rem(me + d, slabs)))
    each(1, cohort, lambda d: greet(barrier, subj=lax.rem(who + d, cohort)))
    greet(barrier, yslab=other)
    greet(barrier, slab=up, yslab=other)
    greet(barrier, slab=down, yslab=other)

    lane = lax.broadcasted_iota(jnp.int32, (8, 128), 1)
    below = core.astype(F32)
    above = 1.0 - below

    def build(z):
        out_low = jnp.logical_and(z < HALO, me == 0)
        out_high = jnp.logical_and(z >= depth + HALO, me == slabs - 1)
        keep = jnp.where(jnp.logical_or(out_low, out_high), 0.0, 1.0)
        for source, places in ((own, ((8, None),)), (peer, ((0, below), (16, above)))):
            plane = source[z].astype(F32) * keep
            a, b = plane[:, :128], plane[:, 128:]
            for move in range(-HALO, HALO + 1):
                if move == 0:
                    ra, rb = a, b
                else:
                    ra = pltpu.roll(a, (-move) % 128, 1)
                    rb = pltpu.roll(b, (-move) % 128, 1)
                    if move < 0:
                        ra, rb = (
                            jnp.where(lane < -move, 0.0, ra),
                            jnp.where(lane < -move, ra, rb),
                        )
                    else:
                        ra, rb = (
                            jnp.where(lane >= 128 - move, rb, ra),
                            jnp.where(lane >= 128 - move, 0.0, rb),
                        )
                for row, factor in places:
                    for half, value in enumerate((ra, rb)):
                        if factor is not None:
                            value = value * factor
                        shifted[move + HALO, z, half, row : row + 8, :] = value

    each(0, depth + 2 * HALO, build)

    def first_warp(z):
        rows = pl.ds(pl.multiple_of(z * 8, 8), 8)
        for half in range(2):
            cols = pl.ds(half * 128, 128)
            shift = []
            for c in range(3):
                value = offsets[c, z, :, cols]
                shift.append(((value & 1) == 1, value >= 0))
            planes = []
            for mz in range(5):
                lines = []
                for my in range(5):
                    values = [shifted[mx, z + mz, half, 6 + my : 14 + my, :] for mx in range(5)]
                    lines.append(list(pick(shift[2], values)))
                low, high = pick_many(shift[1], lines)
                planes.append(low + high)
            low, high = pick_many(shift[0], planes)
            found = low + high
            lows = found[0::2]
            steps = [found[2 * i + 1] - found[2 * i] for i in range(4)]
            for i in range(4):
                corners[i, rows, cols] = lows[i]
                corners[4 + i, rows, cols] = steps[i]
            u = [u0[c, rows, cols] for c in range(3)]
            value, slopes = warp(lows, steps, u, template[rows, cols])
            warped[rows, cols] = value
            for c in range(3):
                grad[c, rows, cols] = slopes[c]

    each(0, depth, first_warp)
    pl.semaphore_wait(barrier, slabs - 1 + cohort - 1 + 3)

    def part_of(ref, p):
        return ref.at[pl.ds(pl.multiple_of(p * share, share), share)]

    def scatter(it, source, slots):
        def copy(d):
            p = lax.rem(who + d, cohort)
            return send(
                part_of(source, p), slots.at[who], rs_send.at[it, d], rs_recv.at[it, who], subj=p
            )

        each(1, cohort, lambda d: copy(d).start())

        def recv():
            def one(d):
                p = lax.rem(who + d, cohort)
                send(
                    part_of(source, p), slots.at[p], rs_send.at[it, d], rs_recv.at[it, p], subj=p
                ).wait()

            each(1, cohort, one)

        return recv

    def spread(it, source, slots):
        each(
            1,
            cohort,
            lambda d: send(
                source, slots.at[who], tg_send.at[it, d], tg_recv.at[it, who],
                subj=lax.rem(who + d, cohort),
            ).start(),
        )

        def recv():
            def one(d):
                p = lax.rem(who + d, cohort)
                send(source, slots.at[p], tg_send.at[it, d], tg_recv.at[it, p], subj=p).wait()

            each(1, cohort, one)

        return recv

    def adjoint(it):
        for c in range(3):
            high, low = split(grad[c])
            first = dot(high, bx[...]) + dot(low, bx[...])
            high, low = split(first)
            part = dot(wa[...], jnp.concatenate([high, high, low], axis=0)) * SCALE
            cols = pl.ds(c * 128, 128)
            for g in range(3):
                terms[it, 3 * core + g, :, cols] = part[16 * g : 16 * g + 16].astype(BF16)

    def exchange(it):
        mine_rows = terms.at[it, pl.ds(3 * core, 3)]
        peer_rows = terms.at[it, pl.ds(3 * other, 3)]
        lower = terms.at[it, 3 * core]
        upper = terms.at[it, 3 * core + 1]
        plan = [
            (upper, 6, core, dict(slab=up)),
            (upper, 6, core, dict(slab=up, yslab=other)),
            (lower, 8, core, dict(slab=down)),
            (lower, 8, core, dict(slab=down, yslab=other)),
        ]
        outs = [
            send(src, terms.at[it, slot + k], ex_send.at[it, i], ex_recv.at[it, i], **where)
            for i, (src, slot, k, where) in enumerate(plan)
        ]
        ins = [
            send(src, terms.at[it, slot + k], ex_send.at[it, i], ex_recv.at[it, i], **where)
            for i, (src, slot, k, where) in enumerate(
                [
                    (upper, 6, core, dict(slab=up)),
                    (upper, 6, other, dict(slab=up, yslab=other)),
                    (lower, 8, core, dict(slab=down)),
                    (lower, 8, other, dict(slab=down, yslab=other)),
                ]
            )
        ]
        across = send(mine_rows, mine_rows, ex_send.at[it, 4], ex_recv.at[it, 4], yslab=other)
        back = send(mine_rows, peer_rows, ex_send.at[it, 4], ex_recv.at[it, 4], yslab=other)
        for copy in outs + [across]:
            copy.start()

        def recv():
            for copy in ins + [back]:
                copy.wait()

        return recv

    def reduce_terms(it):
        edge = jnp.where(me == 0, 1, jnp.where(me == slabs - 1, 2, 0))
        chosen = gather[edge]
        total = dot(chosen, terms[it].reshape(160, 384))
        grid[...] = total
        for q in range(4):
            parts[it, q] = total[16 * q : 16 * q + 16].astype(BF16)
        squares = total * total
        squares = squares[:, :128] + squares[:, 128:256] + squares[:, 256:]
        peak = jnp.sqrt(jnp.max(squares, axis=(0, 1), keepdims=True))
        mine[it] = jnp.broadcast_to(peak, (1, 128))

    def send_peaks(it):
        peaks[it, me] = mine[it]

        def start(d):
            slab = lax.rem(me + slabs - d, slabs)
            send(mine.at[it], peaks.at[it, me], pk_send.at[it, d], pk_recv.at[it, me], slab=slab).start()

        each(1, slabs, start)

        def recv():
            def one(d):
                slab = lax.rem(me + slabs - d, slabs)
                send(
                    mine.at[it], peaks.at[it, slab], pk_send.at[it, d], pk_recv.at[it, slab], slab=slab
                ).wait()

            each(1, slabs, one)
            peak = jnp.max(peaks[it], axis=0)
            return STEP / (peak + TINY)

        return recv

    def send_grid(it):
        block = parts.at[it, core]
        tail = parts.at[it, 2 + core]
        slot = 2 * me + core
        end = 2 * slabs + core
        last = me == slabs - 1

        def order(d):
            half = lax.div(d, 2)
            far = slabs // 2
            up_way = lax.rem(me + far - half, slabs)
            down_way = lax.rem(me + slabs - far + half, slabs)
            return jnp.where(lax.rem(d, 2) == 0, up_way, down_way)

        def start(d):
            slab = order(d)
            send(block, pieces.at[it, slot], ag_send.at[it, d], ag_recv.at[it, me], slab=slab).start()

        def start_tail(d):
            slab = order(d)
            send(tail, pieces.at[it, end], tl_send.at[it, d], tl_recv.at[it, 0], slab=slab).start()

        pieces[it, slot] = parts[it, core]

        @pl.when(last)
        def _():
            pieces[it, end] = parts[it, 2 + core]

        across = send(block, pieces.at[it, slot], fw_send.at[it, me], fw_recv.at[it, me], yslab=other)
        start(0)
        each(2, slabs, start)

        @pl.when(last)
        def _():
            start_tail(0)
            each(2, slabs, start_tail)

        across.start()

        def forward(d):
            slab = order(slabs + 1 - d)
            src = pieces.at[it, 2 * slab + core]
            send(block, src, ag_send.at[it, slabs + 1 - d], ag_recv.at[it, slab], slab=slab).wait()
            send(src, src, fw_send.at[it, slab], fw_recv.at[it, slab], yslab=other).start()

        def finish(d):
            slab = lax.rem(me + d, slabs)
            src = pieces.at[it, 2 * slab + core]
            dst = pieces.at[it, 2 * slab + other]
            send(src, dst, fw_send.at[it, slab], fw_recv.at[it, slab], yslab=other).wait()

        def recv():
            each(2, slabs, forward)
            far = order(0)
            src = pieces.at[it, 2 * far + core]
            send(block, src, ag_send.at[it, 0], ag_recv.at[it, far], slab=far).wait()
            send(src, src, fw_send.at[it, far], fw_recv.at[it, far], yslab=other).start()

            @pl.when(jnp.logical_not(last))
            def _():
                send(
                    tail, pieces.at[it, end], tl_send.at[it, 0], tl_recv.at[it, 0], slab=up
                ).wait_recv()

            src = pieces.at[it, end]
            send(src, src, fw_send.at[it, slabs], fw_recv.at[it, slabs], yslab=other).start()

            @pl.when(last)
            def _():
                send(tail, src, tl_send.at[it, 0], tl_recv.at[it, 0], slab=up).wait_send()
                each(
                    2,
                    slabs,
                    lambda d: send(
                        tail, src, tl_send.at[it, d], tl_recv.at[it, 0], slab=up
                    ).wait_send(),
                )

            each(0, slabs, finish)
            dst = pieces.at[it, 2 * slabs + other]
            send(src, dst, fw_send.at[it, slabs], fw_recv.at[it, slabs], yslab=other).wait()

        return recv

    def own_rows(ref):
        return ref[pl.ds(pl.multiple_of(who * share, share), share), :]

    small[...] = warped[...].astype(BF16)
    piece[who] = own_rows(small)
    got_parts = scatter(0, small, piece)
    adjoint(0)
    got_terms = exchange(0)
    got_terms()
    reduce_terms(0)
    got_peaks = send_peaks(0)
    got_grid_1 = send_grid(0)
    field([grid[:, c * 128 : c * 128 + 128] for c in range(3)], wf[core], bxt[...], moved)
    got_parts()
    total = piece[0].astype(F32)
    for p in range(1, cohort):
        total = total + piece[p].astype(F32)
    summed[...] = (total / cohort).astype(BF16)
    means[who] = summed[...]
    got_means = spread(0, summed, means)
    factor_1 = got_peaks()
    got_means()
    for p in range(cohort):
        current[p * share : p * share + share] = means[p].astype(F32)

    def second_warp(z):
        rows = pl.ds(pl.multiple_of(z * 8, 8), 8)
        for half in range(2):
            cols = pl.ds(half * 128, 128)
            lows = [corners[i, rows, cols] for i in range(4)]
            steps = [corners[4 + i, rows, cols] for i in range(4)]
            u = [u0[c, rows, cols] - factor_1 * moved[c, rows, cols] for c in range(3)]
            value, slopes = warp(lows, steps, u, current[rows, cols])
            warped[rows, cols] = value
            for c in range(3):
                grad[c, rows, cols] = slopes[c]

    each(0, depth, second_warp)
    wide[who] = own_rows(warped)
    got_parts = scatter(1, warped, wide)
    adjoint(1)
    got_terms = exchange(1)
    got_terms()
    reduce_terms(1)
    got_peaks = send_peaks(1)
    got_grid_2 = send_grid(1)
    got_parts()
    total = wide[0]
    for p in range(1, cohort):
        total = total + wide[p]
    current[0:share] = total
    wide_means[who] = total
    got_means = spread(1, current.at[pl.ds(0, share)], wide_means)
    got_grid_1()
    factor_2 = got_peaks()
    got_grid_2()

    def combine(t):
        change = factor_1[:, 0:1] * pieces[0, t].astype(F32) + factor_2[:, 0:1] * pieces[1, t].astype(F32)
        for c in range(3):
            for i in range(2):
                delta_out[c, 2 * t + i] = change[8 * i : 8 * i + 8, c * 128 : c * 128 + 128]

    each(0, 2 * slabs + 2, combine)
    got_means()
    for p in range(cohort):
        total_out[p * share : p * share + share] = wide_means[p]


def call(kernel, name, outs, scratch, ident, args, spaces):
    return pl.pallas_call(
        kernel,
        out_shape=outs,
        in_specs=[pl.BlockSpec(memory_space=s) for s in spaces],
        out_specs=[pl.BlockSpec(memory_space=pltpu.VMEM)] * len(outs),
        scratch_shapes=scratch,
        compiler_params=pltpu.CompilerParams(
            collective_id=ident, has_side_effects=True, vmem_limit_bytes=24 * 1024 * 1024
        ),
        name=name,
    )(*args)


def solution(mesh):
    slabs = mesh.shape["slab"]
    cohort = mesh.shape["subj"]
    assert mesh.shape["yslab"] == 2 and slabs >= 4 and slabs % 2 == 0

    def shards(subjects, offsets, template, control):
        depth, height, width = subjects.shape[1:]
        rows = depth * height
        share = rows // cohort
        wf, bxt, bx, wa, gather = constants(depth, height, width, control.shape[4])
        vmem = pltpu.VMEM
        dma = pltpu.SemaphoreType.DMA
        deep = depth + 2 * HALO
        own, peer, u0 = call(
            lambda *refs: halo_kernel(slabs, *refs),
            "halo",
            [
                jax.ShapeDtypeStruct((deep, height, width), BF16),
                jax.ShapeDtypeStruct((deep, height, width), BF16),
                jax.ShapeDtypeStruct((3, rows, width), F32),
            ],
            [
                vmem((deep, height, width), BF16),
                vmem((deep, height, width), BF16),
                vmem((3, 7, 7, 128), F32),
                vmem((3, 8, 8, 128), F32),
                dma,
                dma((5,)),
                dma((5,)),
            ],
            0,
            (subjects[0], control[0], wf, bxt),
            (vmem, pl.ANY, vmem, vmem),
        )
        total, delta = call(
            lambda *refs: main_kernel(slabs, cohort, *refs),
            "main",
            [
                jax.ShapeDtypeStruct((rows, width), F32),
                jax.ShapeDtypeStruct((3, 4 * slabs + 4, 8, 128), F32),
            ],
            [
                vmem((5, deep, 2, 24, 128), F32),
                vmem((8, rows, width), F32),
                vmem((3, rows, width), F32),
                vmem((rows, width), F32),
                vmem((rows, width), F32),
                vmem((3, rows, width), F32),
                vmem((2, 10, 16, 384), BF16),
                vmem((64, 384), F32),
                vmem((2, 4, 16, 384), BF16),
                vmem((rows, width), BF16),
                vmem((cohort, share, width), BF16),
                vmem((share, width), BF16),
                vmem((2, 2 * slabs + 2, 16, 384), BF16),
                vmem((cohort, share, width), BF16),
                vmem((cohort, share, width), F32),
                vmem((cohort, share, width), F32),
                vmem((2, slabs, 1, 128), F32),
                vmem((2, 1, 128), F32),
                dma((2, 5)), dma((2, 5)),
                dma((2, slabs)), dma((2, slabs)),
                dma((2, cohort)), dma((2, cohort)),
                dma((2, cohort)), dma((2, cohort)),
                dma((2, slabs)), dma((2, slabs)),
                dma((2, slabs + 1)), dma((2, slabs + 1)),
                dma((2, slabs)), dma((2, 1)),
            ],
            1,
            (own, peer, u0, offsets[0], template.reshape(rows, width), wf, bxt, bx, wa, gather),
            (vmem,) * 10,
        )
        template_out = (total / cohort).reshape(depth, height, width)
        control_out = control - delta[None, :, : control.shape[2], : control.shape[3], :]
        return template_out, control_out

    in_specs = (
        P(("group", "subj"), "slab", "yslab", None),
        P(("group", "subj"), None, "slab", "yslab", None),
        P(("group", "slab"), "yslab", None),
        P(("group", "subj"), None, None, None, None),
    )
    out_specs = (P(("group", "slab"), "yslab", None), P(("group", "subj"), None, None, None, None))
    return jax.shard_map(shards, mesh=mesh, in_specs=in_specs, out_specs=out_specs, check_vma=False)
```

time: 248 us -> 96.6 us (0.39)
  the two profiles are of different devices: /device:TPU:82 before, /device:TPU:65 now
where the time goes in v1:
time: 96.6 us; the launch traced here: 96.5 us
  Pallas kernels  92 us (95%)
  local copies, waits for them, and re-layouts  2.88 us (3%)
    pallas_call x2, Pallas kernels, call(): pl.pallas_call(kernel, out_shape=outs, in_specs=[pl.BlockSpec(memory_spac...  92 us

profile of v1, /device:TPU:65, one launch (start us, length us, event | category | flops | bytes accessed | tf_op | source)
XLA Modules:
  0.0 96.5 jit_solution(10485336296262491843)
XLA Ops:
  0.6 0.0 copy-start
  0.6 0.0 copy-start.1
  0.7 0.0 copy-start.5
  0.7 1.2 %copy.20 = f32[1,3,67,7,128]{4,3,2,1,0:T(8,128)S(1)} copy(f32[1,3,67,7,128]{4,0,3,2,1:T(1,128)} %param.12) | data formatting | bytes 1440768 | tf_op jit(solution)/shard_map/squeeze | solution.py:617
  1.9 0.0 copy-done
  1.9 0.0 copy-done.1
  1.9 0.0 copy-done.5
  1.9 0.0 copy-start.2
  1.9 0.0 copy-start.3
  1.9 0.0 copy-start.4
  2.0 0.0 copy-start.6
  2.0 0.0 copy-start.7
  2.0 46.9 %halo.1 = (bf16[20,8,256]{2,1,0:T(8,128)(2,1)S(1)}, bf16[20,8,256]{2,1,0:T(8,128)(2,1)S(1)}, f32[3,128,256]{2,1,0:T(8,128)S(1)}) custom-call(bf16[16,8,256]{2,1,0:T(8,128)(2,1)S(1)} %bitcast.14, f32[3,67,7,128]{3,2,1,0:T(8,128)S(1)} %bitcast.11, bf16[2,128,192]{2,1,0:T(8,128)(2,1)S(1)} %copy-done.1, bf16[256,256]{1,0:T(8,128)(2,1)S(1)} %copy-done), custom_call_target="tpu_custom_call" | custom-call | tf_op jit(solution)/shard_map/halo/pallas_call | solution.py:573
  48.9 0.0 copy-done.2
  48.9 0.0 copy-done.3
  48.9 0.0 copy-done.4
  48.9 0.0 copy-done.6
  49.0 0.0 copy-done.7
  49.0 0.0 copy-start.8
  49.0 45.1 %main.1 = (f32[128,256]{1,0:T(8,128)S(1)}, f32[3,68,8,128]{3,2,1,0:T(8,128)S(1)}) custom-call(bf16[20,8,256]{2,1,0:T(8,128)(2,1)S(1)} %get-tuple-element.7.refs_0_, bf16[20,8,256]{2,1,0:T(8,128)(2,1)S(1)} %get-tuple-element.8.refs_1_, f32[3,128,256]{2,1,0:T(8,128)S(1)} %get-tuple-element.9.refs_2_, s32[3,16,8,256]{3,2,1,0:T(8,128)S(1)} %bitcast.12, ...), custom_call_target="tpu_custom_call" | custom-call | tf_op jit(solution)/shard_map/main/pallas_call | solution.py:573
  94.1 0.7 multiply_bitcast_fusion
  94.7 0.0 copy-done.8
  94.7 0.1 copy_subtract_fusion
  94.9 1.6 %copy.16 = f32[1,3,67,7,128]{4,0,3,2,1:T(1,128)} copy(f32[1,3,67,7,128]{4,3,2,1,0:T(8,128)S(1)} %copy_subtract_fusion) | data formatting | bytes 1440768
Async XLA Ops:
  0.6 1.3 %copy-start = (bf16[256,256]{1,0:T(8,128)(2,1)S(1)}, bf16[256,256]{1,0:T(8,128)(2,1)}, u32[]{:S(2)}) copy-start(bf16[256,256]{1,0:T(8,128)(2,1)} %constant.14.clone.refs_3_.refs_6_) | copy-start | bytes 393220
  0.6 1.3 %copy-start.1 = (bf16[2,128,192]{2,1,0:T(8,128)(2,1)S(1)}, bf16[2,128,192]{2,1,0:T(8,128)(2,1)}, u32[]{:S(2)}) copy-start(bf16[2,128,192]{2,1,0:T(8,128)(2,1)} %constant.13.clone.refs_2_.refs_5_) | copy-start | bytes 294916
  0.7 1.3 %copy-start.5 = (bf16[1,16,8,256]{3,2,1,0:T(8,128)(2,1)S(1)}, bf16[1,16,8,256]{3,2,1,0:T(8,128)(2,1)}, u32[]{:S(2)}) copy-start(bf16[1,16,8,256]{3,2,1,0:T(8,128)(2,1)} %param.9) | copy-start | bytes 196612
  1.9 47.0 %copy-start.2 = (s32[1,3,16,8,256]{4,3,2,1,0:T(8,128)S(1)}, s32[1,3,16,8,256]{4,3,2,1,0:T(8,128)}, u32[]{:S(2)}) copy-start(s32[1,3,16,8,256]{4,3,2,1,0:T(8,128)} %param.10) | copy-start | bytes 1179652
  1.9 47.0 %copy-start.3 = (f32[16,8,256]{2,1,0:T(8,128)S(1)}, f32[16,8,256]{2,1,0:T(8,128)}, u32[]{:S(2)}) copy-start(f32[16,8,256]{2,1,0:T(8,128)} %param.11) | copy-start | bytes 393220
  1.9 47.0 %copy-start.4 = (bf16[3,64,160]{2,1,0:T(8,128)(2,1)S(1)}, bf16[3,64,160]{2,1,0:T(8,128)(2,1)}, u32[]{:S(2)}) copy-start(bf16[3,64,160]{2,1,0:T(8,128)(2,1)} %constant.17.clone.refs_9_) | copy-start | bytes 184324
  2.0 47.0 %copy-start.6 = (bf16[256,128]{1,0:T(8,128)(2,1)S(1)}, bf16[256,128]{1,0:T(8,128)(2,1)}, u32[]{:S(2)}) copy-start(bf16[256,128]{1,0:T(8,128)(2,1)} %constant.15.clone.refs_7_) | copy-start | bytes 196612
  2.0 47.0 %copy-start.7 = (bf16[48,384]{1,0:T(8,128)(2,1)S(1)}, bf16[48,384]{1,0:T(8,128)(2,1)}, u32[]{:S(2)}) copy-start(bf16[48,384]{1,0:T(8,128)(2,1)} %constant.16.clone.refs_8_) | copy-start | bytes 110596
  49.0 45.8 %copy-start.8 = (f32[1,3,67,7,128]{4,0,3,2,1:T(1,128)S(1)}, f32[1,3,67,7,128]{4,0,3,2,1:T(1,128)}, u32[]{:S(2)}) copy-start(f32[1,3,67,7,128]{4,0,3,2,1:T(1,128)} %param.12) | copy-start | bytes 2161156

commit v2 on v1

v2 whole, which is shorter than its diff:
```python
import jax
import jax.numpy as jnp
import numpy as np
from jax import lax
from jax.experimental import pallas as pl
from jax.experimental.pallas import tpu as pltpu
from jax.sharding import PartitionSpec as P

KNOT = 4
HALO = 2
STEP = 0.5
TINY = 1e-06
CUBE = 384.0
CUBE_X = 48.0
SCALE = 1.0 / (CUBE * CUBE * CUBE_X)
F32 = jnp.float32
BF16 = jnp.bfloat16
MESH = pl.DeviceIdType.MESH


def spline(count, columns, spacing, wrap):
    whole = 6 * spacing**3
    matrix = np.zeros((count, columns))
    for t in range(count):
        j = t // spacing
        s = (t - j * spacing) / spacing
        weights = [
            (1 - s) ** 3 / 6,
            (3 * s**3 - 6 * s**2 + 4) / 6,
            (-3 * s**3 + 3 * s**2 + 3 * s + 1) / 6,
            s**3 / 6,
        ]
        for o in range(4):
            column = (j + o) % columns if wrap else j + o
            matrix[t, column] += weights[o] * whole
    return np.rint(matrix)


def halves(whole):
    high = np.asarray(whole, np.float32).astype(BF16).astype(np.float32)
    low = (whole - high).astype(np.float32)
    assert (low.astype(BF16).astype(np.float32) == low).all()
    return high, low


def constants(depth, height, width, columns_x):
    assert (depth, height) == (16, 8)
    bz = spline(depth, 7, KNOT, False)
    by = spline(height, 5, KNOT, False)
    forward = np.zeros((2, depth, height, 8, 8))
    for k in range(2):
        forward[k, :, :, :7, 2 * k : 2 * k + 5] = np.einsum("za,yb->zyab", bz, by)
    dense = np.zeros((2, 2, depth * height, 64))
    rows = forward[:, :, :, :7, :7].reshape(2, depth * height, 49)
    dense[:, 0, :, :49] = rows
    dense[:, 1, :, 7:56] = rows
    forward = forward.reshape(2, depth * height, 64)
    forward = np.concatenate([dense, forward[:, None]], axis=1)
    high, low = halves(forward)
    forward = np.concatenate([high, low, high], axis=3)
    adjoint = np.zeros((3, 16, depth, height))
    for group, rows in enumerate(([0, 1, 2], [4, 5, 6], [3])):
        for place, a in enumerate(rows):
            for b in range(5):
                adjoint[group, place * 5 + b] = np.outer(bz[:, a], by[:, b])
    adjoint = adjoint.reshape(48, depth * height)
    high, low = halves(adjoint)
    adjoint = np.concatenate([high, low, high], axis=1)
    gather = np.zeros((3, 64, 10, 16))
    for edge in range(3):
        for a in range(7):
            for b in range(7):
                for k in range(2):
                    c = b - 2 * k
                    if not 0 <= c < 5:
                        continue
                    row = a * 8 + b
                    if a < 3:
                        gather[edge, row, 3 * k, a * 5 + c] = 1
                        if edge != 1:
                            gather[edge, row, 6 + k, a * 5 + c] = 1
                    elif a == 3:
                        gather[edge, row, 3 * k + 2, c] = 1
                    else:
                        gather[edge, row, 3 * k + 1, (a - 4) * 5 + c] = 1
                        if edge != 2:
                            gather[edge, row, 8 + k, (a - 4) * 5 + c] = 1
    gather = gather.reshape(3, 64, 160)
    bx = spline(width, columns_x, 2, True)
    across = np.concatenate([bx.T, bx.T], axis=0)
    bx = np.concatenate([bx, bx], axis=0)
    return [jnp.asarray(m, BF16) for m in (forward, across, bx, adjoint, gather)]


def split(x):
    high = x.astype(BF16)
    return high, (x - high.astype(F32)).astype(BF16)


def dot(a, b):
    return jnp.dot(a, b, preferred_element_type=F32)


def field(coeffs, wf, bxt, out):
    high, low = split(coeffs)
    first = dot(wf, jnp.concatenate([high, high, low], axis=0))
    high, low = split(first)
    for c in range(3):
        cols = slice(c * 128, c * 128 + 128)
        out[c] = dot(jnp.concatenate([high[:, cols], low[:, cols]], axis=1), bxt) * SCALE


def send(src, dst, send_sem, recv_sem, **where):
    return pltpu.make_async_remote_copy(
        src_ref=src,
        dst_ref=dst,
        send_sem=send_sem,
        recv_sem=recv_sem,
        device_id=where,
        device_id_type=MESH,
    )


def greet(barrier, **where):
    pl.semaphore_signal(barrier, inc=1, device_id=where, device_id_type=MESH)


def wait_in(ref, sem, **where):
    send(ref, ref, sem, sem, **where).wait_recv()


def wait_out(ref, sem, **where):
    send(ref, ref, sem, sem, **where).wait_send()


def each(first, last, body):
    def step(i, carry):
        body(i)
        return carry

    lax.fori_loop(first, last, step, 0)


def pick(shift, values):
    odd, top = shift
    steps = [jnp.where(odd, values[i + 1], values[i]) for i in range(4)]
    return jnp.where(top, steps[2], steps[0]), jnp.where(top, steps[3], steps[1])


def pick_many(shift, groups):
    pairs = [pick(shift, values) for values in zip(*groups)]
    return [p[0] for p in pairs], [p[1] for p in pairs]


def warp(lows, steps, u, current):
    th = [jnp.tanh(x) for x in u]
    fz, fy, fx = [0.5 + 0.5 * t for t in th]
    along = [low + fx * step for low, step in zip(lows, steps)]
    slope_y = [along[1] - along[0], along[3] - along[2]]
    along_y = [along[0] + fy * slope_y[0], along[2] + fy * slope_y[1]]
    slope_x = [steps[0] + fy * (steps[1] - steps[0]), steps[2] + fy * (steps[3] - steps[2])]
    slopes = [
        along_y[1] - along_y[0],
        slope_y[0] + fz * (slope_y[1] - slope_y[0]),
        slope_x[0] + fz * (slope_x[1] - slope_x[0]),
    ]
    warped = along_y[0] + fz * slopes[0]
    resid = warped - current
    return warped, [resid * slope * (1.0 - t * t) for slope, t in zip(slopes, th)]


def main_kernel(
    slabs, cohort, subject, offsets_in, template_in, control, wf_in, bxt_in, bx_in, wa_in, gather_in,
    mean_out, delta_out,
    own, peer, band, u0, offsets, template, wf, bxt, bx, wa, gather,
    shifted, corners, grad, warped, current, moved, terms, grid,
    small, piece, summed, pieces, means, wide, wide_means, peaks, mine,
    in_sem, halo_sem, know_sem, know_subj_sem, ex_sem, pk_sem, rs_sem, tg_sem, ag_sem, fw_sem,
):
    me = lax.axis_index("slab")
    core = lax.axis_index("yslab")
    who = lax.axis_index("subj")
    other = 1 - core
    depth = offsets.shape[1]
    share = depth // cohort * 8
    far = slabs // 2
    hop = slabs // 4

    def slab_at(d):
        return lax.rem(me + (d + slabs), slabs)

    def subj_at(d):
        return lax.rem(who + (d + cohort), cohort)

    up, down = slab_at(1), slab_at(-1)
    barrier = pltpu.get_barrier_semaphore()
    greet(barrier, yslab=other)
    for slab in (up, down):
        greet(barrier, slab=slab)
        greet(barrier, slab=slab, yslab=other)
    for d in (1, -1):
        greet(barrier, subj=subj_at(d))

    rows_in = control.shape[0] // 3
    begin = jnp.minimum(me * (depth // KNOT * 7), rows_in - 56)
    late = jnp.where(me == slabs - 1, 1, 0)
    inner = pl.ds(HALO, depth)
    fetch_subject = pltpu.make_async_copy(subject, own.at[inner], in_sem.at[0])
    fetch_control = [
        pltpu.make_async_copy(
            control.at[pl.ds(c * rows_in + begin, 56), 0],
            band.at[pl.ds(0, 56), pl.ds(c * 128, 128)],
            in_sem.at[1 + c],
        )
        for c in range(3)
    ]
    fetch_rest = [
        pltpu.make_async_copy(src, dst, in_sem.at[4 + i])
        for i, (src, dst) in enumerate(
            [
                (wf_in.at[core, late], wf.at[0]),
                (bxt_in, bxt),
                (wf_in.at[core, 2], wf.at[1]),
                (offsets_in, offsets),
                (template_in, template),
                (bx_in, bx),
                (wa_in, wa),
                (gather_in, gather),
            ]
        )
    ]
    for copy in [fetch_subject] + fetch_control + fetch_rest:
        copy.start()
    band[56:64, :] = jnp.zeros((8, 384), F32)

    pl.semaphore_wait(barrier, 7)
    fetch_subject.wait()
    low = pl.ds(0, HALO)
    high = pl.ds(depth + HALO, HALO)
    first = pl.ds(HALO, HALO)
    last = pl.ds(depth, HALO)
    across = send(own.at[inner], peer.at[inner], halo_sem.at[0], halo_sem.at[1], yslab=other)
    along = [
        send(own.at[last], own.at[low], halo_sem.at[2], halo_sem.at[3], slab=up),
        send(own.at[first], own.at[high], halo_sem.at[2], halo_sem.at[3], slab=down),
        send(own.at[last], peer.at[low], halo_sem.at[2], halo_sem.at[3], slab=up, yslab=other),
        send(own.at[first], peer.at[high], halo_sem.at[2], halo_sem.at[3], slab=down, yslab=other),
    ]
    for copy in along + [across]:
        copy.start()

    know_slab = [1]
    know_subj = [1]

    def tell():
        if know_slab[0] < far:
            r = know_slab[0].bit_length() - 1
            for d in (know_slab[0], -know_slab[0]):
                greet(know_sem.at[r], slab=slab_at(d))
        if know_subj[0] < cohort // 2:
            r = know_subj[0].bit_length() - 1
            for d in (know_subj[0], -know_subj[0]):
                greet(know_subj_sem.at[r], subj=subj_at(d))

    def learn():
        if know_slab[0] < far:
            pl.semaphore_wait(know_sem.at[know_slab[0].bit_length() - 1], 2)
            know_slab[0] *= 2
        if know_subj[0] < cohort // 2:
            pl.semaphore_wait(know_subj_sem.at[know_subj[0].bit_length() - 1], 2)
            know_subj[0] *= 2

    tell()

    for copy in fetch_control + fetch_rest[:2]:
        copy.wait()
    field(band[...], wf[0], bxt[...], u0)

    lane = lax.broadcasted_iota(jnp.int32, (8, 128), 1)
    below = core.astype(F32)
    above = 1.0 - below

    def build(source, places, z):
        out_low = jnp.logical_and(z < HALO, me == 0)
        out_high = jnp.logical_and(z >= depth + HALO, me == slabs - 1)
        keep = jnp.where(jnp.logical_or(out_low, out_high), 0.0, 1.0)
        plane = source[z].astype(F32) * keep
        a, b = plane[:, :128], plane[:, 128:]
        for move in range(-HALO, HALO + 1):
            if move == 0:
                ra, rb = a, b
            else:
                ra = pltpu.roll(a, (-move) % 128, 1)
                rb = pltpu.roll(b, (-move) % 128, 1)
                if move < 0:
                    ra, rb = (
                        jnp.where(lane < -move, 0.0, ra),
                        jnp.where(lane < -move, ra, rb),
                    )
                else:
                    ra, rb = (
                        jnp.where(lane >= 128 - move, rb, ra),
                        jnp.where(lane >= 128 - move, 0.0, rb),
                    )
            for row, factor in places:
                for half, value in enumerate((ra, rb)):
                    if factor is not None:
                        value = value * factor
                    shifted[move + HALO, z, half, row : row + 8, :] = value

    at_own = ((8, None),)
    at_peer = ((0, below), (16, above))

    def edge_of(i, top):
        return jnp.where(i < HALO, i, i + (top - HALO))

    each(HALO, depth + HALO, lambda z: build(own, at_own, z))
    learn()
    tell()
    across.wait()
    each(HALO, depth + HALO, lambda z: build(peer, at_peer, z))
    for copy in fetch_rest[2:]:
        copy.wait()

    def first_warp(z):
        rows = pl.ds(pl.multiple_of(z * 8, 8), 8)
        for half in range(2):
            cols = pl.ds(half * 128, 128)
            shift = []
            for c in range(3):
                value = offsets[c, z, :, cols]
                shift.append(((value & 1) == 1, value >= 0))
            planes = []
            for mz in range(5):
                lines = []
                for my in range(5):
                    values = [shifted[mx, z + mz, half, 6 + my : 14 + my, :] for mx in range(5)]
                    lines.append(list(pick(shift[2], values)))
                low, high = pick_many(shift[1], lines)
                planes.append(low + high)
            low, high = pick_many(shift[0], planes)
            found = low + high
            lows = found[0::2]
            steps = [found[2 * i + 1] - found[2 * i] for i in range(4)]
            for i in range(4):
                corners[i, rows, cols] = lows[i]
                corners[4 + i, rows, cols] = steps[i]
            u = [u0[c, rows, cols] for c in range(3)]
            value, slopes = warp(lows, steps, u, template[rows, cols])
            warped[rows, cols] = value
            for c in range(3):
                grad[c, rows, cols] = slopes[c]

    each(HALO, depth - HALO, first_warp)
    learn()
    tell()
    planes = own.at[pl.ds(0, 4 * HALO)]
    wait_in(planes, halo_sem.at[3], slab=up)
    wait_out(planes, halo_sem.at[2], slab=up)

    def build_edge(i):
        z = edge_of(i, depth + HALO)
        build(own, at_own, z)
        build(peer, at_peer, z)

    each(0, 2 * HALO, build_edge)
    each(0, 2 * HALO, lambda i: first_warp(edge_of(i, depth - HALO)))
    while know_subj[0] < cohort // 2:
        learn()
        tell()

    def part_of(ref, p):
        return ref.at[pl.ds(pl.multiple_of(p * share, share), share)]

    def own_rows(ref):
        return ref[pl.ds(pl.multiple_of(who * share, share), share), :]

    others = [d for d in range(1, cohort)]

    def scatter(it, source, slots):
        for d in others:
            p = subj_at(d)
            send(part_of(source, p), slots.at[who], rs_sem.at[it, 0], rs_sem.at[it, 1], subj=p).start()

    def spread(it, source, slots):
        for d in others:
            send(source, slots.at[who], tg_sem.at[it, 0], tg_sem.at[it, 1], subj=subj_at(d)).start()

    def got(it, slots, sem):
        several = slots.at[pl.ds(0, cohort - 1)]
        wait_in(several, sem.at[it, 1], subj=subj_at(1))
        wait_out(several, sem.at[it, 0], subj=subj_at(1))

    def adjoint(it):
        firsts = []
        for c in range(3):
            high, low = split(grad[c])
            firsts.append(dot(jnp.concatenate([high, low], axis=1), bx[...]))
        high, low = split(jnp.concatenate(firsts, axis=1))
        part = dot(wa[...], jnp.concatenate([high, high, low], axis=0)) * SCALE
        for g in range(3):
            terms[it, 3 * core + g] = part[16 * g : 16 * g + 16].astype(BF16)

    def exchange(it):
        mine_rows = terms.at[it, pl.ds(3 * core, 3)]
        lower = terms.at[it, 3 * core]
        upper = terms.at[it, 3 * core + 1]
        sems = (ex_sem.at[it, 0], ex_sem.at[it, 1])
        send(upper, terms.at[it, 6 + core], *sems, slab=up, yslab=other).start()
        send(lower, terms.at[it, 8 + core], *sems, slab=down, yslab=other).start()
        send(upper, terms.at[it, 6 + core], *sems, slab=up).start()
        send(lower, terms.at[it, 8 + core], *sems, slab=down).start()
        send(mine_rows, mine_rows, *sems, yslab=other).start()

    def got_exchange(it):
        several = terms.at[it, pl.ds(0, 7)]
        wait_in(several, ex_sem.at[it, 1], yslab=other)
        wait_out(several, ex_sem.at[it, 0], yslab=other)

    def reduce_terms(it):
        edge = jnp.where(me == 0, 1, jnp.where(me == slabs - 1, 2, 0))
        total = dot(gather[edge], terms[it].reshape(160, 384))
        squares = total * total
        squares = squares[:, :128] + squares[:, 128:256] + squares[:, 256:]
        peak = jnp.sqrt(jnp.max(squares, axis=(0, 1), keepdims=True))
        mine[...] = jnp.broadcast_to(peak, (1, 128))
        p0 = peak.astype(BF16).astype(F32)
        p1 = (peak - p0).astype(BF16).astype(F32)
        p2 = peak - p0 - p1
        wide_peak = jnp.concatenate([jnp.broadcast_to(p, (64, 128)) for p in (p0, p1, p2)], axis=1)
        row = lax.broadcasted_iota(jnp.int32, (64, 384), 0)
        packed = jnp.where((row & 7) == 7, wide_peak, total).astype(BF16)
        grid[...] = total
        lowest = packed[0:16], packed[32:48]
        highest = packed[16:32], packed[48:64]
        pieces[it, core, me] = jnp.where(core == 0, lowest[0], highest[0])

        @pl.when(me == slabs - 1)
        def _():
            pieces[it, core, slabs] = jnp.where(core == 0, lowest[1], highest[1])

    def send_peaks():
        peaks[me] = mine[...]
        for i in range(slabs - 1):
            d = far if i == 0 else (far - (i + 1) // 2) * (1 if i % 2 else -1)
            send(mine, peaks.at[me], pk_sem.at[0], pk_sem.at[1], slab=slab_at(d)).start()

    def got_peaks():
        several = peaks.at[pl.ds(0, slabs - 1)]
        wait_in(several, pk_sem.at[1], slab=up)
        wait_out(several, pk_sem.at[0], slab=up)
        return STEP / (jnp.max(peaks[...], axis=0) + TINY)

    end = slabs - 1

    def blocks(it, origin, count):
        return pieces.at[it, core, pl.ds(origin, count)]

    def ship(it, origin, sent, targets):
        for ends, count in ((origin == end, 2), (origin != end, 1)):

            @pl.when(ends)
            def _():
                ref = blocks(it, origin, count)
                for d, place in targets:
                    send(ref, ref, ag_sem.at[it, sent], ag_sem.at[it, place], slab=slab_at(d)).start()

    def settle(it, count, extra, origins, wait, place):
        found = origins[0] == end
        for origin in origins[1:]:
            found = jnp.logical_or(found, origin == end)
        for case, number in ((found, count + extra), (jnp.logical_not(found), count)):

            @pl.when(case)
            def _():
                wait(blocks(it, 0, number), ag_sem.at[it, place], slab=up)

    OWN, EDGE_UP, EDGE_DOWN, NEAR, FAR, GO_UP, GO_DOWN = range(7)

    def send_grid(it):
        targets = [(hop, EDGE_UP), (-hop, EDGE_DOWN)]
        for d in range(hop - 1, 0, -1):
            targets += [(d, NEAR), (-d, NEAR)]
        ship(it, me, OWN, targets)

    def hand_on(it):
        origin = slab_at(-hop)
        settle(it, 1, 1, [origin], wait_in, EDGE_UP)
        ship(it, origin, GO_UP, [(d, FAR) for d in range(hop, 0, -1)])
        origin = slab_at(hop)
        settle(it, 1, 1, [origin], wait_in, EDGE_DOWN)
        ship(it, origin, GO_DOWN, [(-d, FAR) for d in range(hop - 1, 0, -1)])

    def got_grid(it):
        near = [slab_at(d) for d in range(1 - hop, hop) if d != 0]
        if near:
            settle(it, len(near), 1, near, wait_in, NEAR)
        distant = [slab_at(d) for d in range(hop + 1, slabs - hop)]
        settle(it, len(distant), 1, distant, wait_in, FAR)
        both = pieces.at[it, core]
        send(both, both, fw_sem.at[it, 0], fw_sem.at[it, 1], yslab=other).start()

    def sent_grid(it):
        both = pieces.at[it, core]
        send(both, both, fw_sem.at[it, 0], fw_sem.at[it, 1], yslab=other).wait()
        for origin, count, sent in (
            (me, 2 * hop, OWN),
            (slab_at(-hop), hop, GO_UP),
            (slab_at(hop), hop - 1, GO_DOWN),
        ):
            if count:
                settle(it, count, count, [origin], wait_out, sent)

    small[...] = warped[...].astype(BF16)
    piece[who] = own_rows(small)
    scatter(0, small, piece)
    adjoint(0)
    exchange(0)
    while know_slab[0] < far:
        learn()
        tell()
    got_exchange(0)
    reduce_terms(0)
    send_peaks()
    send_grid(0)
    field(grid[...], wf[1], bxt[...], moved)
    got(0, piece, rs_sem)
    total = piece[0].astype(F32)
    for p in range(1, cohort):
        total = total + piece[p].astype(F32)
    summed[...] = (total / cohort).astype(BF16)
    means[who] = summed[...]
    spread(0, summed, means)
    hand_on(0)
    factor_1 = got_peaks()
    got(0, means, tg_sem)
    for p in range(cohort):
        current[p * share : p * share + share] = means[p].astype(F32)

    def second_warp(z):
        rows = pl.ds(pl.multiple_of(z * 8, 8), 8)
        for half in range(2):
            cols = pl.ds(half * 128, 128)
            lows = [corners[i, rows, cols] for i in range(4)]
            steps = [corners[4 + i, rows, cols] for i in range(4)]
            u = [u0[c, rows, cols] - factor_1 * moved[c, rows, cols] for c in range(3)]
            value, slopes = warp(lows, steps, u, current[rows, cols])
            warped[rows, cols] = value
            for c in range(3):
                grad[c, rows, cols] = slopes[c]

    each(0, depth, second_warp)
    wide[who] = own_rows(warped)
    adjoint(1)
    exchange(1)
    scatter(1, warped, wide)
    got_exchange(1)
    reduce_terms(1)
    send_grid(1)
    got_grid(0)
    got(1, wide, rs_sem)
    total = wide[0]
    for p in range(1, cohort):
        total = total + wide[p]
    total = total / cohort
    current[0:share] = total
    wide_means[who] = total
    spread(1, current.at[pl.ds(0, share)], wide_means)
    hand_on(1)
    sent_grid(0)
    got_grid(1)
    got(1, wide_means, tg_sem)
    for p in range(cohort):
        mean_out[p * share : p * share + share] = wide_means[p]
    sent_grid(1)

    peak = None
    for k in range(2):
        for slab in range(slabs):
            row = pieces[1, k, slab, 7:8, :].astype(F32)
            row = (row[:, :128] + row[:, 128:256]) + row[:, 256:]
            peak = row if peak is None else jnp.maximum(peak, row)
    factor_2 = STEP / (peak + TINY)
    grid_rows = delta_out.shape[0] // 21
    sub = lax.broadcasted_iota(jnp.int32, (8, 128), 0)
    made = {}

    def change(s):
        if s not in made:
            c, a = divmod(s, grid_rows)
            cols = slice(c * 128, c * 128 + 128)
            k, slab, i = (a // 2) % 2, a // 4, a % 2
            one, two = (
                pieces[it, k, slab, :, cols].astype(F32)[8 * i : 8 * i + 8] for it in range(2)
            )
            made[s] = factor_1 * one + factor_2 * two
        return made[s]

    for t in range((3 * grid_rows * 7 + 7) // 8):
        s, skip = divmod(8 * t, 7)
        value = change(s)
        if skip:
            value = pltpu.roll(value, 8 - skip, 0)
        if s + 1 < 3 * grid_rows:
            after = change(s + 1)
            if skip < 6:
                pass
            after = pltpu.roll(after, 7 - skip, 0)
            value = jnp.where(sub < 7 - skip, value, after)
            delta_out[8 * t : 8 * t + 8, :] = value
        else:
            delta_out[8 * t : 8 * t + 7 - skip, :] = value[0 : 7 - skip]
        made.pop(s - 1, None)


def solution(mesh):
    slabs = mesh.shape["slab"]
    cohort = mesh.shape["subj"]
    assert mesh.shape["yslab"] == 2 and slabs >= 4 and slabs % 4 == 0

    def shards(subjects, offsets, template, control):
        depth, height, width = subjects.shape[1:]
        rows = depth * height
        share = rows // cohort
        wf, bxt, bx, wa, gather = constants(depth, height, width, control.shape[4])
        vmem = pltpu.VMEM
        dma = pltpu.SemaphoreType.DMA
        plain = pltpu.SemaphoreType.REGULAR
        deep = depth + 2 * HALO
        grid_rows = control.shape[2]
        rounds = (slabs // 2).bit_length() - 1
        args = (
            subjects[0],
            offsets[0],
            template.reshape(rows, width),
            control.reshape(3 * grid_rows * 7, 1, 128),
            wf, bxt, bx, wa, gather,
        )
        mean, delta = pl.pallas_call(
            lambda *refs: main_kernel(slabs, cohort, *refs),
            out_shape=[
                jax.ShapeDtypeStruct((rows, width), F32),
                jax.ShapeDtypeStruct((3 * grid_rows * 7, 128), F32),
            ],
            in_specs=[pl.BlockSpec(memory_space=pl.ANY)] * len(args),
            out_specs=[pl.BlockSpec(memory_space=vmem)] * 2,
            scratch_shapes=[
                vmem((deep, height, width), BF16),
                vmem((deep, height, width), BF16),
                vmem((64, 384), F32),
                vmem((3, rows, width), F32),
                vmem((3, depth, height, width), jnp.int32),
                vmem((rows, width), F32),
                vmem((2, *wf.shape[2:]), BF16),
                vmem(bxt.shape, BF16),
                vmem(bx.shape, BF16),
                vmem(wa.shape, BF16),
                vmem(gather.shape, BF16),
                vmem((5, deep, 2, 24, 128), F32),
                vmem((8, rows, width), F32),
                vmem((3, rows, width), F32),
                vmem((rows, width), F32),
                vmem((rows, width), F32),
                vmem((3, rows, width), F32),
                vmem((2, 10, 16, 384), BF16),
                vmem((64, 384), F32),
                vmem((rows, width), BF16),
                vmem((cohort, share, width), BF16),
                vmem((share, width), BF16),
                vmem((2, 2, slabs + 1, 16, 384), BF16),
                vmem((cohort, share, width), BF16),
                vmem((cohort, share, width), F32),
                vmem((cohort, share, width), F32),
                vmem((slabs, 1, 128), F32),
                vmem((1, 128), F32),
                dma((12,)),
                dma((4,)),
                plain((rounds,)),
                plain((max((cohort // 2).bit_length() - 1, 1),)),
                dma((2, 2)),
                dma((2,)),
                dma((2, 2)),
                dma((2, 2)),
                dma((2, 7)),
                dma((2, 2)),
            ],
            compiler_params=pltpu.CompilerParams(
                collective_id=0, has_side_effects=True, vmem_limit_bytes=48 * 1024 * 1024
            ),
            name="register",
        )(*args)
        return mean.reshape(depth, height, width), control - delta.reshape(control.shape)

    in_specs = (
        P(("group", "subj"), "slab", "yslab", None),
        P(("group", "subj"), None, "slab", "yslab", None),
        P(("group", "slab"), "yslab", None),
        P(("group", "subj"), None, None, None, None),
    )
    out_specs = (P(("group", "slab"), "yslab", None), P(("group", "subj"), None, None, None, None))
    return jax.shard_map(shards, mesh=mesh, in_specs=in_specs, out_specs=out_specs, check_vma=False)
```

time: 96.6 us -> 91.6 us (0.948)
  Pallas kernels: 92 us -> 78.7 us
  local copies, waits for them, and re-layouts: 2.88 us -> 11.7 us
    pallas_call x2 -> x1, Pallas kernels: 92 us -> 78.7 us  [shards(): pl.pallas_call(lambda *refs: main_kernel(slabs, cohort, *refs), out_shape...]
    unnamed x19 -> x22, local copies, waits for them, and re-layouts: 1.66 us -> 11.6 us
    squeeze x1 -> x0, local copies, waits for them, and re-layouts: 1.22 us -> none  [shards(): control[0]]
where the time goes in v2:
time: 91.6 us; the launch traced here: 91.1 us
  Pallas kernels  78.7 us (86%)
  local copies, waits for them, and re-layouts  11.7 us (13%)
    pallas_call x1, Pallas kernels, shards(): pl.pallas_call(lambda *refs: main_kernel(slabs, cohort, *refs), out_shape...  78.7 us
    unnamed x22, local copies, waits for them, and re-layouts  11.6 us

profile of v2, /device:TPU:65, one launch (start us, length us, event | category | flops | bytes accessed | tf_op | source)
XLA Modules:
  0.0 91.1 jit_solution(16036662898618514450)
XLA Ops:
  0.6 0.0 copy-start
  0.6 1.1 %copy-done = f32[1,3,67,7,128]{4,0,3,2,1:T(1,128)S(1)} copy-done((f32[1,3,67,7,128]{4,0,3,2,1:T(1,128)S(1)}, f32[1,3,67,7,128]{4,0,3,2,1:T(1,128)}, u32[]{:S(2)}) %copy-start) | copy-done | bytes 720408
  1.7 0.0 copy-start.2
  1.7 1.0 %copy-done.2 = s32[1,3,16,8,256]{4,3,2,1,0:T(8,128)S(1)} copy-done((s32[1,3,16,8,256]{4,3,2,1,0:T(8,128)S(1)}, s32[1,3,16,8,256]{4,3,2,1,0:T(8,128)}, u32[]{:S(2)}) %copy-start.2) | copy-done | bytes 393240
  2.7 0.0 copy-start.3
  2.7 1.0 %copy-done.3 = bf16[2,3,128,192]{3,2,1,0:T(8,128)(2,1)S(1)} copy-done((bf16[2,3,128,192]{3,2,1,0:T(8,128)(2,1)S(1)}, bf16[2,3,128,192]{3,2,1,0:T(8,128)(2,1)}, u32[]{:S(2)}) %copy-start.3) | copy-done | bytes 294936
  3.7 0.0 copy-start.4
  3.7 0.9 copy-done.4
  4.6 0.0 copy-start.5
  4.6 0.9 copy-done.5
  5.5 0.0 copy-start.6
  5.5 0.9 copy-done.6
  6.5 0.0 copy-start.7
  6.5 0.9 copy-done.7
  7.3 0.0 copy-start.8
  7.3 0.8 copy-done.8
  8.2 0.0 copy-start.9
  8.2 0.8 copy-done.9
  9.0 78.7 %register.1 = (f32[128,256]{1,0:T(8,128)S(1)}, f32[1407,128]{1,0:T(8,128)S(1)}) custom-call(bf16[16,8,256]{2,1,0:T(8,128)(2,1)S(1)} %bitcast.9, s32[3,16,8,256]{3,2,1,0:T(8,128)S(1)} %bitcast.6, f32[128,256]{1,0:T(8,128)S(1)} %bitcast.7, f32[1407,1,128]{2,1,0:T(1,128)S(1)} %bitcast.5, bf16[2,3,128,192]{3,2,1,0:T(8,128)(2,1)S(1)} %copy-done.3, ...), custom_call_target="tpu_custom_call" | custom-call | tf_op jit(solution)/shard_map/register/pallas_call | solution.py:639
  87.6 0.0 copy-start.1
  87.6 0.1 reshape.19
  87.8 1.0 %copy-done.1 = f32[1,3,67,7,128]{4,0,3,2,1:T(1,128)S(1)} copy-done((f32[1,3,67,7,128]{4,0,3,2,1:T(1,128)S(1)}, f32[1,3,67,7,128]{4,0,3,2,1:T(1,128)}, u32[]{:S(2)}) %copy-start.1) | copy-done | bytes 720408
  88.8 0.1 copy_subtract_fusion
  88.9 1.6 %copy.13 = f32[1,3,67,7,128]{4,0,3,2,1:T(1,128)} copy(f32[1,3,67,7,128]{4,3,2,1,0:T(8,128)S(1)} %copy_subtract_fusion) | data formatting | bytes 1440768
  90.5 0.7 copy.16
Async XLA Ops:
  0.6 1.1 %copy-start = (f32[1,3,67,7,128]{4,0,3,2,1:T(1,128)S(1)}, f32[1,3,67,7,128]{4,0,3,2,1:T(1,128)}, u32[]{:S(2)}) copy-start(f32[1,3,67,7,128]{4,0,3,2,1:T(1,128)} %param.12) | copy-start | bytes 2161156
  1.7 1.0 %copy-start.2 = (s32[1,3,16,8,256]{4,3,2,1,0:T(8,128)S(1)}, s32[1,3,16,8,256]{4,3,2,1,0:T(8,128)}, u32[]{:S(2)}) copy-start(s32[1,3,16,8,256]{4,3,2,1,0:T(8,128)} %param.10) | copy-start | bytes 1179652
  2.7 1.0 %copy-start.3 = (bf16[2,3,128,192]{3,2,1,0:T(8,128)(2,1)S(1)}, bf16[2,3,128,192]{3,2,1,0:T(8,128)(2,1)}, u32[]{:S(2)}) copy-start(bf16[2,3,128,192]{3,2,1,0:T(8,128)(2,1)} %constant.10.clone.refs_4_) | copy-start | bytes 884740
  3.7 0.9 copy-start.4
  4.6 0.9 copy-start.5
  5.5 0.9 copy-start.6
  6.5 0.9 copy-start.7
  7.3 0.8 copy-start.8
  8.2 0.8 copy-start.9
  87.6 1.1 %copy-start.1 = (f32[1,3,67,7,128]{4,0,3,2,1:T(1,128)S(1)}, f32[1,3,67,7,128]{4,0,3,2,1:T(1,128)}, u32[]{:S(2)}) copy-start(f32[1,3,67,7,128]{4,0,3,2,1:T(1,128)} %param.12) | copy-start | bytes 2161156

commit v3 on v2

--- a/solution.py
+++ b/solution.py
@@ -121,6 +121,16 @@
     )
 
 
+def by_groups(first, last, size, body):
+    assert (last - first) % size == 0
+
+    def group(i):
+        for j in range(size):
+            body(first + i * size + j)
+
+    each(0, (last - first) // size, group)
+
+
 def greet(barrier, **where):
     pl.semaphore_signal(barrier, inc=1, device_id=where, device_id_type=MESH)
 
@@ -171,10 +181,10 @@
 
 def main_kernel(
     slabs, cohort, subject, offsets_in, template_in, control, wf_in, bxt_in, bx_in, wa_in, gather_in,
-    mean_out, delta_out,
+    mean_out, bulk_out, rest_out,
     own, peer, band, u0, offsets, template, wf, bxt, bx, wa, gather,
     shifted, corners, grad, warped, current, moved, terms, grid,
-    small, piece, summed, pieces, means, wide, wide_means, peaks, mine,
+    small, piece, summed, pieces, means, wide, wide_means, peaks, mine, bulk, rest,
     in_sem, halo_sem, know_sem, know_subj_sem, ex_sem, pk_sem, rs_sem, tg_sem, ag_sem, fw_sem,
 ):
     me = lax.axis_index("slab")
@@ -226,6 +236,8 @@
                 (bx_in, bx),
                 (wa_in, wa),
                 (gather_in, gather),
+                (control.at[pl.ds(0, bulk.shape[0]), 0], bulk),
+                (control.at[pl.ds(bulk.shape[0], rest.shape[0])], rest),
             ]
         )
     ]
@@ -314,12 +326,12 @@
     def edge_of(i, top):
         return jnp.where(i < HALO, i, i + (top - HALO))
 
-    each(HALO, depth + HALO, lambda z: build(own, at_own, z))
+    by_groups(HALO, depth + HALO, 4, lambda z: build(own, at_own, z))
     learn()
     tell()
     across.wait()
-    each(HALO, depth + HALO, lambda z: build(peer, at_peer, z))
-    for copy in fetch_rest[2:]:
+    by_groups(HALO, depth + HALO, 4, lambda z: build(peer, at_peer, z))
+    for copy in fetch_rest[2:-2]:
         copy.wait()
 
     def first_warp(z):
@@ -363,7 +375,7 @@
         build(own, at_own, z)
         build(peer, at_peer, z)
 
-    each(0, 2 * HALO, build_edge)
+    by_groups(0, 2 * HALO, 2, build_edge)
     each(0, 2 * HALO, lambda i: first_warp(edge_of(i, depth - HALO)))
     while know_subj[0] < cohort // 2:
         learn()
@@ -477,11 +489,15 @@
 
     OWN, EDGE_UP, EDGE_DOWN, NEAR, FAR, GO_UP, GO_DOWN = range(7)
 
-    def send_grid(it):
-        targets = [(hop, EDGE_UP), (-hop, EDGE_DOWN)]
+    def send_edges(it):
+        ship(it, me, OWN, [(hop, EDGE_UP), (-hop, EDGE_DOWN)])
+
+    def send_near(it):
+        targets = []
         for d in range(hop - 1, 0, -1):
             targets += [(d, NEAR), (-d, NEAR)]
-        ship(it, me, OWN, targets)
+        if targets:
+            ship(it, me, OWN, targets)
 
     def hand_on(it):
         origin = slab_at(-hop)
@@ -522,8 +538,7 @@
     got_exchange(0)
     reduce_terms(0)
     send_peaks()
-    send_grid(0)
-    field(grid[...], wf[1], bxt[...], moved)
+    send_edges(0)
     got(0, piece, rs_sem)
     total = piece[0].astype(F32)
     for p in range(1, cohort):
@@ -531,6 +546,8 @@
     summed[...] = (total / cohort).astype(BF16)
     means[who] = summed[...]
     spread(0, summed, means)
+    field(grid[...], wf[1], bxt[...], moved)
+    send_near(0)
     hand_on(0)
     factor_1 = got_peaks()
     got(0, means, tg_sem)
@@ -549,14 +566,14 @@
             for c in range(3):
                 grad[c, rows, cols] = slopes[c]
 
-    each(0, depth, second_warp)
+    by_groups(0, depth, 2, second_warp)
     wide[who] = own_rows(warped)
     adjoint(1)
     exchange(1)
     scatter(1, warped, wide)
     got_exchange(1)
     reduce_terms(1)
-    send_grid(1)
+    send_edges(1)
     got_grid(0)
     got(1, wide, rs_sem)
     total = wide[0]
@@ -566,6 +583,7 @@
     current[0:share] = total
     wide_means[who] = total
     spread(1, current.at[pl.ds(0, share)], wide_means)
+    send_near(1)
     hand_on(1)
     sent_grid(0)
     got_grid(1)
@@ -581,7 +599,9 @@
             row = (row[:, :128] + row[:, 128:256]) + row[:, 256:]
             peak = row if peak is None else jnp.maximum(peak, row)
     factor_2 = STEP / (peak + TINY)
-    grid_rows = delta_out.shape[0] // 21
+    for copy in fetch_rest[-2:]:
+        copy.wait()
+    grid_rows = control.shape[0] // 21
     sub = lax.broadcasted_iota(jnp.int32, (8, 128), 0)
     made = {}
 
@@ -602,15 +622,28 @@
         if skip:
             value = pltpu.roll(value, 8 - skip, 0)
         if s + 1 < 3 * grid_rows:
-            after = change(s + 1)
-            if skip < 6:
-                pass
-            after = pltpu.roll(after, 7 - skip, 0)
+            after = pltpu.roll(change(s + 1), 7 - skip, 0)
             value = jnp.where(sub < 7 - skip, value, after)
-            delta_out[8 * t : 8 * t + 8, :] = value
+            rows = pl.ds(8 * t, 8)
+            bulk_out[rows, :] = bulk[rows, :] - value
         else:
-            delta_out[8 * t : 8 * t + 7 - skip, :] = value[0 : 7 - skip]
+            for j in range(rest.shape[0]):
+                rest_out[j] = rest[j] - value[j : j + 1]
         made.pop(s - 1, None)
+
+
+def write_kernel(mean, bulk, rest, mean_out, control_out, sems):
+    copies = [
+        pltpu.make_async_copy(bulk, control_out.at[pl.ds(0, bulk.shape[0]), 0], sems.at[0]),
+        pltpu.make_async_copy(
+            rest, control_out.at[pl.ds(bulk.shape[0], rest.shape[0])], sems.at[1]
+        ),
+        pltpu.make_async_copy(mean, mean_out, sems.at[2]),
+    ]
+    for copy in copies:
+        copy.start()
+    for copy in copies:
+        copy.wait()
 
 
 def solution(mesh):
@@ -629,21 +662,25 @@
         deep = depth + 2 * HALO
         grid_rows = control.shape[2]
         rounds = (slabs // 2).bit_length() - 1
+        dense = control.reshape(3 * grid_rows * 7, 1, 128)
+        left = dense.shape[0] % 8
+        assert left
         args = (
             subjects[0],
             offsets[0],
             template.reshape(rows, width),
-            control.reshape(3 * grid_rows * 7, 1, 128),
+            dense,
             wf, bxt, bx, wa, gather,
         )
-        mean, delta = pl.pallas_call(
+        mean, bulk, rest = pl.pallas_call(
             lambda *refs: main_kernel(slabs, cohort, *refs),
             out_shape=[
                 jax.ShapeDtypeStruct((rows, width), F32),
-                jax.ShapeDtypeStruct((3 * grid_rows * 7, 128), F32),
+                jax.ShapeDtypeStruct((dense.shape[0] - left, 128), F32),
+                jax.ShapeDtypeStruct((left, 1, 128), F32),
             ],
-            in_specs=[pl.BlockSpec(memory_space=pl.ANY)] * len(args),
-            out_specs=[pl.BlockSpec(memory_space=vmem)] * 2,
+            in_specs=[pl.BlockSpec(memory_space=pltpu.HBM)] * len(args),
+            out_specs=[pl.BlockSpec(memory_space=vmem)] * 3,
             scratch_shapes=[
                 vmem((deep, height, width), BF16),
                 vmem((deep, height, width), BF16),
@@ -673,7 +710,9 @@
                 vmem((cohort, share, width), F32),
                 vmem((slabs, 1, 128), F32),
                 vmem((1, 128), F32),
-                dma((12,)),
+                vmem((dense.shape[0] - left, 128), F32),
+                vmem((left, 1, 128), F32),
+                dma((14,)),
                 dma((4,)),
                 plain((rounds,)),
                 plain((max((cohort // 2).bit_length() - 1, 1),)),
@@ -688,8 +727,20 @@
                 collective_id=0, has_side_effects=True, vmem_limit_bytes=48 * 1024 * 1024
             ),
             name="register",
-        )(*args)
-        return mean.reshape(depth, height, width), control - delta.reshape(control.shape)
+        )(*[pltpu.with_memory_space_constraint(a, pltpu.HBM) for a in args])
+        mean, dense = pl.pallas_call(
+            write_kernel,
+            out_shape=[
+                jax.ShapeDtypeStruct((rows, width), F32),
+                jax.ShapeDtypeStruct(dense.shape, F32),
+            ],
+            in_specs=[pl.BlockSpec(memory_space=vmem)] * 3,
+            out_specs=[pl.BlockSpec(memory_space=pltpu.HBM)] * 2,
+            scratch_shapes=[dma((3,))],
+            compiler_params=pltpu.CompilerParams(vmem_limit_bytes=4 * 1024 * 1024),
+            name="write",
+        )(mean, bulk, rest)
+        return mean.reshape(depth, height, width), dense.reshape(control.shape)
 
     in_specs = (
         P(("group", "subj"), "slab", "yslab", None),

time: 91.6 us -> 80 us (0.87)
  local copies, waits for them, and re-layouts: 11.7 us -> 0 us
    unnamed x22 -> x0, local copies, waits for them, and re-layouts: 11.6 us -> none
    pallas_call x0 -> x1, Pallas kernels: none -> 0.92 us  [shards(): pl.pallas_call(write_kernel, out_shape=[jax.ShapeDtypeStruct((rows, width...]
where the time goes in v3:
time: 80 us; the launch traced here: 79.9 us
  Pallas kernels  79.3 us (99%)
    pallas_call x1, Pallas kernels, shards(): pl.pallas_call(lambda *refs: main_kernel(slabs, cohort, *refs), out_shape...  78.3 us

profile of v3, /device:TPU:65, one launch (start us, length us, event | category | flops | bytes accessed | tf_op | source)
XLA Modules:
  0.0 79.9 jit_solution(6310522664362941987)
XLA Ops:
  0.6 78.3 %register.1 = (f32[128,256]{1,0:T(8,128)S(1)}, f32[1400,128]{1,0:T(8,128)S(1)}, f32[7,1,128]{2,1,0:T(1,128)S(1)}) custom-call(bf16[16,8,256]{2,1,0:T(8,128)(2,1)} %bitcast.9, s32[3,16,8,256]{3,2,1,0:T(8,128)} %bitcast.7, f32[128,256]{1,0:T(8,128)} %bitcast.8, f32[1407,1,128]{2,1,0:T(1,128)} %bitcast.6, bf16[2,3,128,192]{3,2,1,0:T(8,128)(2,1)} %constant.10.clone.refs_4_, ...), custom_call_target="tpu_custom_call" | custom-call | tf_op jit(solution)/shard_map/register/pallas_call | solution.py:675
  79.0 0.9 %write.1 = (f32[128,256]{1,0:T(8,128)}, f32[1407,1,128]{2,1,0:T(1,128)}) custom-call(f32[128,256]{1,0:T(8,128)S(1)} %get-tuple-element.7.mean, f32[1400,128]{1,0:T(8,128)S(1)} %get-tuple-element.8.bulk, f32[7,1,128]{2,1,0:T(1,128)S(1)} %get-tuple-element.9.rest), custom_call_target="tpu_custom_call" | custom-call | tf_op jit(solution)/shard_map/write/pallas_call | solution.py:731
